TPU v7x, 16 devices: a whole 2x2x2 slice. The times are simulated.
16 devices in a mesh: dp: 2 (over z), tp: 8 (over y, x, core).
Axes of the slice: x: 2, y: 2, z: 2, core: 2. Of those that a mesh axis runs over, the one named last changes fastest.
Arguments:
- x_in: bfloat16 [256, 4096], P('dp'), parts along dimension 0
- tok_pos: int32 [256], P('dp'), parts along dimension 0
- self_k: bfloat16 [256, 64, 64, 64], P('dp', None, 'tp'), parts along dimension 0
- self_v: bfloat16 [256, 64, 64, 64], P('dp', None, 'tp'), parts along dimension 0
- cross_k: bfloat16 [256, 128, 64, 64], P('dp', None, 'tp'), parts along dimension 0
- cross_v: bfloat16 [256, 128, 64, 64], P('dp', None, 'tp'), parts along dimension 0
- enc_mask: int32 [256, 128], P('dp'), parts along dimension 0
- rel_bias: float32 [32, 64], P(None, 'tp')
- w_q: bfloat16 [4096, 4096], P(None, 'tp')
- w_k: bfloat16 [4096, 4096], P(None, 'tp')
- w_v: bfloat16 [4096, 4096], P(None, 'tp')
- w_o: bfloat16 [4096, 4096], P('tp')
- cross_q: bfloat16 [4096, 4096], P(None, 'tp')
- cross_o: bfloat16 [4096, 4096], P('tp')
- w_gate: bfloat16 [4096, 10240], P(None, 'tp')
- w_up: bfloat16 [4096, 10240], P(None, 'tp')
- w_down: bfloat16 [10240, 4096], P('tp')
- norm_self: bfloat16 [4096], replicated
- norm_cross: bfloat16 [4096], replicated
- norm_mlp: bfloat16 [4096], replicated
Outputs:
- output 1: bfloat16 [256, 4096], P('dp'), parts along dimension 0
- output 2: bfloat16 [256, 64, 64, 64], P('dp', None, 'tp'), parts along dimension 0
- output 3: bfloat16 [256, 64, 64, 64], P('dp', None, 'tp'), parts along dimension 0
There are 2 independent parts. A program takes and returns all parts, laid end to end along the dimension named above; an argument that names none is the same for every part.
All inputs are finite; a program needn't handle non-finite values.
Results may differ from a plain program's by a relative error of at most 0.0192555.
Values are sent between devices in bfloat16 or wider.
A program may use at most 1 GiB of HBM per device.

v0:
```python
import math
import jax
import jax.numpy as jnp
from jax import lax
from jax.sharding import PartitionSpec as P

BUCKET_EDGES = tuple(int(math.ceil(16.0 * 8.0 ** (bucket_step / 16.0))) for bucket_step in range(1, 16))
NEG_FILL = -1e30


def rms_norm(values, norm_scale):
    inv_rms = lax.rsqrt(jnp.mean(values * values, axis=-1, keepdims=True) + 1e-6)
    return (values * inv_rms * norm_scale.astype(jnp.float32)).astype(jnp.bfloat16)


def project(normed, weight):
    return jnp.dot(normed, weight, preferred_element_type=jnp.float32).astype(jnp.bfloat16)


def rel_bucket(distance):
    bucket_edges = jnp.array(BUCKET_EDGES, dtype=jnp.int32)
    far_bucket = 16 + jnp.sum((distance[..., None] >= bucket_edges).astype(jnp.int32), axis=-1)
    return jnp.where(distance < 16, distance, far_bucket)


def attend(queries, keys_all, values_all, extra):
    scores = jnp.einsum('bhk,bthk->bht', queries, keys_all, preferred_element_type=jnp.float32) + extra
    probs_bf = jax.nn.softmax(scores, axis=-1).astype(jnp.bfloat16)
    mixed_out = jnp.einsum('bht,bthk->bhk', probs_bf, values_all, preferred_element_type=jnp.float32)
    return mixed_out.astype(jnp.bfloat16)


def self_terms(tok_pos, rel_bias, t_len):
    key_index = jnp.arange(t_len)
    at_pos = (key_index[None, :] == tok_pos[:, None])[:, :, None, None]
    distance = jnp.maximum(tok_pos[:, None] - key_index[None, :], 0)
    bias_rows = jnp.swapaxes(jnp.take(rel_bias, rel_bucket(distance), axis=0), 1, 2)
    causal = (key_index[None, :] <= tok_pos[:, None])[:, None, :]
    return at_pos, jnp.where(causal, bias_rows, NEG_FILL)


def solution(mesh):
    def tp_sum(partial_out):
        return lax.psum(partial_out.astype(jnp.bfloat16), 'tp').astype(jnp.float32)

    def local_layer(x_in, tok_pos, self_k, self_v, cross_k, cross_v, enc_mask, rel_bias, w_q, w_k, w_v, w_o, cross_q, cross_o, w_gate, w_up, w_down, norm_self, norm_cross, norm_mlp):
        row_count, t_len, head_count, head_dim = self_k.shape
        head_shape = (row_count, head_count, head_dim)
        flat_dim = head_count * head_dim
        residual = x_in.astype(jnp.float32)
        normed = rms_norm(residual, norm_self)
        queries = project(normed, w_q).reshape(head_shape)
        new_keys = project(normed, w_k).reshape(head_shape)
        new_values = project(normed, w_v).reshape(head_shape)
        at_pos, self_extra = self_terms(tok_pos, rel_bias, t_len)
        new_self_k = jnp.where(at_pos, new_keys[:, None], self_k)
        new_self_v = jnp.where(at_pos, new_values[:, None], self_v)
        mixed_self = attend(queries, new_self_k, new_self_v, self_extra)
        residual = residual + tp_sum(jnp.dot(mixed_self.reshape(row_count, flat_dim), w_o, preferred_element_type=jnp.float32))
        normed = rms_norm(residual, norm_cross)
        cross_queries = project(normed, cross_q).reshape(head_shape)
        cross_extra = jnp.where(enc_mask[:, None, :] != 0, 0.0, NEG_FILL)
        mixed_cross = attend(cross_queries, cross_k, cross_v, cross_extra)
        residual = residual + tp_sum(jnp.dot(mixed_cross.reshape(row_count, flat_dim), cross_o, preferred_element_type=jnp.float32))
        normed = rms_norm(residual, norm_mlp)
        gate_pre = jnp.dot(normed, w_gate, preferred_element_type=jnp.float32)
        up_pre = jnp.dot(normed, w_up, preferred_element_type=jnp.float32)
        hidden = (jax.nn.gelu(gate_pre, approximate=True) * up_pre).astype(jnp.bfloat16)
        residual = residual + tp_sum(jnp.dot(hidden, w_down, preferred_element_type=jnp.float32))
        return residual.astype(jnp.bfloat16), new_self_k, new_self_v

    cache_spec = P('dp', None, 'tp', None)
    split_cols = P(None, 'tp')
    split_rows = P('tp', None)
    in_specs = (P('dp', None), P('dp'), cache_spec, cache_spec, cache_spec, cache_spec, P('dp', None), split_cols, split_cols, split_cols, split_cols, split_rows, split_cols, split_rows, split_cols, split_cols, split_rows, P(None), P(None), P(None))
    out_specs = (P('dp', None), cache_spec, cache_spec)
    return jax.shard_map(local_layer, mesh=mesh, in_specs=in_specs, out_specs=out_specs, check_vma=False)
```

profile of v0, /device:TPU:0, one launch (start us, length us, event | category | flops | bytes accessed | tf_op | source)
XLA Modules:
  0.0 303.0 jit_solution(3608066473941016882)
XLA Ops:
  7.2 0.7 subtract_maximum_fusion
  8.0 0.8 convert_reduce_fusion
  8.7 0.7 iota_compare_fusion
  9.4 0.7 compare_select_fusion
  10.1 1.5 fusion.5
  11.6 0.7 convert_element_type.73
  12.3 0.8 copy.41
  13.5 3.3 %convolution_convert_fusion.5 = bf16[128,512]{1,0:T(8,128)(2,1)S(1)} fusion(bf16[4096,512]{1,0:T(8,128)(2,1)} %param.30, bf16[128,4096]{1,0:T(8,128)(2,1)} %param.21, f32[4096]{0:T(1024)S(1)} %convert_element_type.73, f32[128]{0:T(128)S(1)} %add_rsqrt_fusion.2), kind=kOutput, calls=%fused_computation.38 | convolution fusion | flops 539033600 | bytes 5390848 | tf_op jit(solution)/shard_map/dot_general | solution.py:17
  17.0 2.9 convolution_convert_fusion.4
  20.0 2.9 convolution_convert_fusion.6
  23.1 11.5 %multiply_reduce_fusion.1 = (f32[128,8,64]{0,1,2:T(8,128)S(1)}, bf16[128,64,8,64]{0,3,2,1:T(8,128)(2,1)}) fusion(f32[128,8,64]{0,2,1:T(8,128)S(1)} %bitcast_convert_fusion.1, bf16[128,64,8,64]{0,3,2,1:T(8,128)(2,1)} %param.23, bf16[128,8,64]{0,2,1:T(8,128)(2,1)S(1)} %bitcast.50, pred[128,64]{0,1:T(8,128)(4,1)S(1)} %get-tuple-element.9), kind=kLoop, calls=%fused_computation.6 | loop fusion | flops 16711680 | bytes 17440768
  34.7 4.3 %copy.50 = f32[128,8,64]{1,2,0:T(8,128)} copy(f32[128,8,64]{0,1,2:T(8,128)S(1)} %get-tuple-element.5) | data formatting | bytes 524288 | tf_op jit(solution)/shard_map/bhk,bthk->bht/dot_general | solution.py:27
  39.0 27.7 %gather_fusion = f32[8192,8]{1,0:T(8,128)} fusion(f32[32,8]{1,0:T(8,128)S(1)} %copy.41, s32[8192]{0:T(1024)S(1)} %broadcast_clamp_fusion), kind=kCustom, calls=%fused_computation | custom fusion | bytes 557056 | tf_op jit(solution)/shard_map/jit(_take)/gather | solution.py:37
  66.7 6.9 %fusion.8 = f32[128,8,64]{1,2,0:T(8,128)} fusion(f32[128,8,64]{1,2,0:T(8,128)} %copy.50, f32[128,64,8]{2,1,0:T(8,128)} %bitcast.48, pred[128,64]{1,0:T(8,128)(4,1)S(1)} %copy.39, pred[128,64]{1,0:T(8,128)(4,1)S(1)} %copy.38), kind=kOutput, calls=%fused_computation.29 | output fusion | flops 460926 | bytes 802816 | tf_op jit(solution)/shard_map/div | solution.py:28
  73.6 3.7 %copy.62 = f32[128,8,64]{0,1,2:T(8,128)S(1)} copy(f32[128,8,64]{1,2,0:T(8,128)} %fusion.8) | data formatting | bytes 524288
  77.3 11.0 %multiply_reduce_fusion = (bf16[128,8,64]{0,2,1:T(8,128)(2,1)S(1)}, bf16[128,64,8,64]{0,3,2,1:T(8,128)(2,1)}) fusion(f32[128,8,64]{0,1,2:T(8,128)S(1)} %copy.62, bf16[128,64,8,64]{0,3,2,1:T(8,128)(2,1)} %param.24, bf16[128,8,64]{0,2,1:T(8,128)(2,1)S(1)} %bitcast.49, pred[128,64]{0,1:T(8,128)(4,1)S(1)} %get-tuple-element.9), kind=kLoop, calls=%fused_computation.5 | loop fusion | flops 16711680 | bytes 17309696 | tf_op jit(solution)/shard_map/bht,bthk->bhk/dot_general | solution.py:29
  88.3 3.9 %convolution_convert_fusion.2 = bf16[128,4096]{1,0:T(8,128)(2,1)} fusion(bf16[128,512]{0,1:T(8,128)(2,1)S(1)} %bitcast.51, bf16[512,4096]{1,0:T(8,128)(2,1)} %param.32), kind=kOutput, calls=%fused_computation.11 | convolution fusion | flops 537395200 | bytes 5373952 | tf_op jit(solution)/shard_map/dot_general | solution.py:59
  92.3 51.7 %all-reduce.4.cloned.1.call-done = bf16[128,4096]{1,0:T(8,128)(2,1)} async-done(((bf16[128,4096]{1,0:T(8,128)(2,1)}), bf16[128,4096]{1,0:T(8,128)(2,1)}) %all-reduce.4.cloned.1.call-update) | async-done | bytes 1048592 | tf_op jit(solution)/shard_map/psum | solution.py:44
  144.1 1.6 multiply_reduce_fusion.3
  145.7 3.3 %convolution_convert_fusion.3 = bf16[128,512]{1,0:T(8,128)(2,1)S(1)} fusion(bf16[4096,512]{1,0:T(8,128)(2,1)} %param.33, bf16[128,4096]{1,0:T(8,128)(2,1)} %all-reduce.4.cloned.1.call-done, bf16[128,4096]{1,0:T(8,128)(2,1)S(1)} %copy-done, f32[4096]{0:T(1024)S(1)} %convert_element_type.83, f32[128]{0:T(128)S(1)} %add_rsqrt_fusion.1), kind=kOutput, calls=%fused_computation.36 | convolution fusion | flops 540082176 | bytes 6439424 | tf_op jit(solution)/shard_map/dot_general | solution.py:17
  149.2 0.7 copy.57
  149.9 8.0 %fusion.43 = f32[128,8,1,128]{3,2,1,0:T(1,128)S(1)} fusion(bf16[128,8,64,1]{2,3,1,0:T(2,128)(2,1)S(1)} %copy.57, bf16[128,128,8,64]{1,3,2,0:T(8,128)(2,1)} %param.25), kind=kOutput, calls=%fused_computation.81 | convolution fusion | flops 16777216 | bytes 17432576 | tf_op jit(solution)/shard_map/bhk,bthk->bht/dot_general | solution.py:27
  158.3 12.3 %fusion.24 = bf16[128,8,1,64]{3,2,1,0:T(2,128)(2,1)S(1)} fusion(bf16[128,128,8,64]{1,3,2,0:T(8,128)(2,1)} %param.26, bf16[128,8,128,1]{2,1,0,3:T(8,128)(2,1)S(1)} %fusion.14), kind=kOutput, calls=%fused_computation.50 | convolution fusion | flops 16777216 | bytes 17170432 | tf_op jit(solution)/shard_map/bht,bthk->bhk/dot_general | solution.py:29
  170.6 0.4 copy.60
  171.0 3.9 %convolution_convert_fusion.1 = bf16[128,4096]{1,0:T(8,128)(2,1)} fusion(bf16[128,512]{0,1:T(8,128)(2,1)S(1)} %bitcast.53, bf16[512,4096]{1,0:T(8,128)(2,1)} %param.34), kind=kOutput, calls=%fused_computation.10 | convolution fusion | flops 537395200 | bytes 5373952 | tf_op jit(solution)/shard_map/dot_general | solution.py:64
  175.0 48.3 %all-reduce.6.cloned.1.call-done = bf16[128,4096]{1,0:T(8,128)(2,1)} async-done(((bf16[128,4096]{1,0:T(8,128)(2,1)}), bf16[128,4096]{1,0:T(8,128)(2,1)}) %all-reduce.6.cloned.1.call-update) | async-done | bytes 1048592 | tf_op jit(solution)/shard_map/psum | solution.py:44
  223.2 1.8 multiply_reduce_fusion.2
  225.0 1.8 multiply_convert_fusion
  226.8 6.4 %fusion.44 = f32[128,1280]{1,0:T(8,128)} fusion(bf16[128,4096]{1,0:T(8,128)(2,1)S(1)} %multiply_convert_fusion, bf16[4096,1280]{1,0:T(8,128)(2,1)} %param.35), kind=kOutput, calls=%fused_computation.82 | convolution fusion | flops 1342177280 | bytes 12189696 | tf_op jit(solution)/shard_map/dot_general | solution.py:66
  233.2 11.7 %convolution_convert_fusion = bf16[128,4096]{1,0:T(8,128)(2,1)} fusion(bf16[1280,4096]{1,0:T(8,128)(2,1)} %param.37, bf16[128,4096]{1,0:T(8,128)(2,1)S(1)} %multiply_convert_fusion, bf16[4096,1280]{1,0:T(8,128)(2,1)} %param.36, f32[128,1280]{1,0:T(8,128)} %fusion.44), kind=kOutput, calls=%fused_computation.9 | convolution fusion | flops 2686517248 | bytes 23724032 | tf_op jit(solution)/shard_map/dot_general | solution.py:69
  244.9 48.3 %all-reduce.8.cloned.1.call-done = bf16[128,4096]{1,0:T(8,128)(2,1)} async-done(((bf16[128,4096]{1,0:T(8,128)(2,1)}), bf16[128,4096]{1,0:T(8,128)(2,1)}) %all-reduce.8.cloned.1.call-update) | async-done | bytes 1048592 | tf_op jit(solution)/shard_map/psum | solution.py:44
  293.3 3.2 %add_convert_fusion = bf16[128,4096]{1,0:T(8,128)(2,1)} fusion(bf16[128,4096]{1,0:T(8,128)(2,1)} %all-reduce.8.cloned.1.call-done, bf16[128,4096]{1,0:T(8,128)(2,1)} %all-reduce.6.cloned.1.call-done, bf16[128,4096]{1,0:T(8,128)(2,1)S(1)} %copy-done.1, bf16[128,4096]{1,0:T(8,128)(2,1)S(1)} %copy-done), kind=kLoop, calls=%fused_computation.23 | loop fusion | flops 4194304 | bytes 5242880 | tf_op jit(solution)/shard_map/convert_element_type | solution.py:70
  (33 shorter events, 1.5 us)
Async XLA Ops:
  7.2 9.8 %copy-start = (bf16[128,4096]{1,0:T(8,128)(2,1)S(1)}, bf16[128,4096]{1,0:T(8,128)(2,1)}, u32[]{:S(2)}) copy-start(bf16[128,4096]{1,0:T(8,128)(2,1)} %param.21) | copy-start | bytes 3145732
  7.2 136.9 %all-reduce.4.cloned.1.call-start = ((), (), s32[]{:S(2)}) async-start(), calls=%async_computation | async-start | bytes 2097152 | tf_op jit(solution)/shard_map/psum | solution.py:44
  88.3 4.0 %copy-start.3 = (bf16[4096]{0:T(1024)(128)(2,1)S(1)}, bf16[4096]{0:T(1024)(128)(2,1)}, u32[]{:S(2)}) copy-start(bf16[4096]{0:T(1024)(128)(2,1)} %param.39) | copy-start | bytes 24580
  88.3 4.0 %copy-start.2 = (s32[128,128]{1,0:T(8,128)S(1)}, s32[128,128]{1,0:T(8,128)}, u32[]{:S(2)}) copy-start(s32[128,128]{1,0:T(8,128)} %param.27) | copy-start | bytes 196612
  92.2 131.0 %all-reduce.6.cloned.1.call-start = ((), (), s32[]{:S(2)}) async-start(), calls=%async_computation.1 | async-start | bytes 2097152 | tf_op jit(solution)/shard_map/psum | solution.py:44
  170.5 4.4 %copy-start.4 = (bf16[4096]{0:T(1024)(128)(2,1)S(1)}, bf16[4096]{0:T(1024)(128)(2,1)}, u32[]{:S(2)}) copy-start(bf16[4096]{0:T(1024)(128)(2,1)} %param.40) | copy-start | bytes 24580
  170.6 52.7 %copy-start.1 = (bf16[128,4096]{1,0:T(8,128)(2,1)S(1)}, bf16[128,4096]{1,0:T(8,128)(2,1)}, u32[]{:S(2)}) copy-start(bf16[128,4096]{1,0:T(8,128)(2,1)} %all-reduce.4.cloned.1.call-done) | copy-start | bytes 3145732
  174.9 118.4 %all-reduce.8.cloned.1.call-start = ((), (), s32[]{:S(2)}) async-start(), calls=%async_computation.2 | async-start | bytes 2097152 | tf_op jit(solution)/shard_map/psum | solution.py:44
Sparse Core Ops, SparseCore 0:
  92.4 51.6 all-reduce.3
  175.0 48.1 all-reduce.5
  245.1 48.1 all-reduce.7
where the time goes:
time: 304 us; the launch traced here: 303 us
  waiting for transfers between devices  148 us (49%)
  matrix products  58.7 us (19%)
  other arithmetic  43.3 us (14%)
  local copies, waits for them, and re-layouts  38.5 us (13%)
  between operations  14 us (5%)
    psum x3, waiting for transfers between devices, tp_sum(): return lax.psum(partial_out.astype(jnp.bfloat16), 'tp').astype(jnp.float32)  148 us
    gather x1, local copies, waits for them, and re-layouts, self_terms(): jnp.take(rel_bias, rel_bucket(distance), axis=0)  27.7 us
    dot_general x4, matrix products, project(): jnp.dot(normed, weight, preferred_element_type=jnp.float32)  12.4 us
    dot_general x1, matrix products, attend(): jnp.einsum('bht,bthk->bhk', probs_bf, values_all, preferred_element_type=...  12.3 us
    dot_general x1, matrix products, local_layer(): jnp.dot(hidden, w_down, preferred_element_type=jnp.float32)  11.7 us
    unnamed x2, other arithmetic  11.6 us
    dot_general x1, other arithmetic, attend(): jnp.einsum('bht,bthk->bhk', probs_bf, values_all, preferred_element_type=...  11 us
    dot_general x1, matrix products, attend(): jnp.einsum('bhk,bthk->bht', queries, keys_all, preferred_element_type=jnp...  8.04 us
  transfers between devices with their start and end apart: 3, of which 3 were waited for; matrix products, arithmetic and copies ran while one was open for 0% of the time, Pallas kernels for 0%

commit v1 on v0

v1 whole, which is shorter than its diff:
```python
import math
import jax
import jax.numpy as jnp
import numpy as np
from jax import lax
from jax.experimental import pallas as pl
from jax.experimental.pallas import tpu as pltpu
from jax.sharding import PartitionSpec as P

F32 = jnp.float32
BF16 = jnp.bfloat16
BUCKET_EDGES = tuple(int(math.ceil(16.0 * 8.0 ** (bucket_step / 16.0))) for bucket_step in range(1, 16))
NEG_FILL = -1e30
ROWS, T_LEN, S_LEN, HEADS, HEAD_DIM = 128, 64, 128, 8, 64
D_MODEL, FLAT, UNITS = 4096, 512, 1280
K_CHUNK = 1024
N_CHUNK = D_MODEL // K_CHUNK


def rms_norm(values, norm_scale):
    inv_rms = lax.rsqrt(jnp.mean(values * values, axis=-1, keepdims=True) + 1e-6)
    return (values * inv_rms * norm_scale).astype(BF16)


def bias_table(rel_bias_t, tok_row):
    step = lax.broadcasted_iota(jnp.int32, (T_LEN, 32), 0)
    bucket = lax.broadcasted_iota(jnp.int32, (T_LEN, 32), 1)
    distance = (T_LEN - 1) - step
    far = jnp.full_like(distance, 16)
    for edge in BUCKET_EDGES:
        far = far + (distance >= edge).astype(jnp.int32)
    own_bucket = jnp.where(distance < 16, distance, far)
    one_hot = (bucket == own_bucket).astype(F32)
    by_step = lax.dot_general(one_hot, rel_bias_t, (((1,), (1,)), ((), ())),
                              precision=lax.Precision.HIGHEST, preferred_element_type=F32)
    shift = (T_LEN - 1) - tok_row
    position = lax.broadcasted_iota(jnp.int32, (T_LEN, ROWS), 0)
    allowed = position <= tok_row
    tables = []
    for head in range(HEADS):
        table = jnp.broadcast_to(by_step[:, head:head + 1], (T_LEN, ROWS))
        for bit in (32, 16, 8, 4, 2, 1):
            moved = jnp.concatenate([table[bit:], table[:bit]], axis=0)
            table = jnp.where((shift & bit) != 0, moved, table)
        tables.append(jnp.where(allowed, table, NEG_FILL))
    return tables


def self_kernel(x_hbm, tok_ref, rel_ref, norm_ref, wq, wk, wv, wo, sk, sv,
                part_ref, nk, nv,
                x_buf, h_buf, w_buf, wo_buf, k_buf, v_buf, acc, q_t, kn_t, vn_t, bias, probs, mix,
                x_sem, w_sem, wo_sem, k_sem, v_sem, ko_sem, vo_sem):
    x_copy = pltpu.make_async_copy(x_hbm, x_buf, x_sem)
    x_copy.start()
    srcs = (wq, wk, wv)

    def w_copy(chunk, which):
        rows = pl.ds(pl.multiple_of(chunk * K_CHUNK, K_CHUNK), K_CHUNK)
        return pltpu.make_async_copy(srcs[which].at[rows, :], w_buf.at[rows, pl.ds(which * FLAT, FLAT)],
                                     w_sem.at[chunk, which])

    def in_copy(src, buf, sem, head):
        return pltpu.make_async_copy(src.at[:, head], buf.at[head], sem.at[head])

    def out_copy(buf, dst, sem, head):
        return pltpu.make_async_copy(buf.at[head], dst.at[:, head], sem.at[head])

    for chunk in range(N_CHUNK):
        for which in range(3):
            w_copy(chunk, which).start()

    def start_in(head, carry):
        in_copy(sk, k_buf, k_sem, head).start()
        in_copy(sv, v_buf, v_sem, head).start()
        return carry
    lax.fori_loop(0, HEADS, start_in, 0)
    wo_copy = pltpu.make_async_copy(wo, wo_buf, wo_sem)
    wo_copy.start()

    tok_row = tok_ref[...]
    for head, table in enumerate(bias_table(rel_ref[...], tok_row)):
        bias[head] = table

    x_copy.wait()

    def norm_rows(step, carry):
        rows = pl.ds(pl.multiple_of(step * 16, 16), 16)
        h_buf[rows, :] = rms_norm(x_buf[rows, :].astype(F32), norm_ref[...].astype(F32))
        return carry
    lax.fori_loop(0, ROWS // 16, norm_rows, 0)

    acc[...] = jnp.zeros_like(acc)

    def qkv_step(chunk, carry):
        for which in range(3):
            w_copy(chunk, which).wait()
            rows = pl.ds(pl.multiple_of(chunk * K_CHUNK, K_CHUNK), K_CHUNK)
            cols = slice(which * FLAT, (which + 1) * FLAT)
            acc[:, cols] += jnp.dot(h_buf[:, rows], w_buf[rows, cols], preferred_element_type=F32)
        return carry
    lax.fori_loop(0, N_CHUNK, qkv_step, 0)

    for which, dst in enumerate((q_t, kn_t, vn_t)):
        for block in range(FLAT // 128):
            start = which * FLAT + block * 128
            turned = jnp.transpose(acc[:, start:start + 128])
            dst[block * 128:(block + 1) * 128, :] = turned.astype(BF16).astype(dst.dtype)

    tok_b = jnp.broadcast_to(tok_row.astype(F32), (HEAD_DIM, ROWS)).astype(BF16)

    def head_step(head, carry):
        lanes = pl.ds(pl.multiple_of(head * HEAD_DIM, HEAD_DIM), HEAD_DIM)
        in_copy(sk, k_buf, k_sem, head).wait()
        query = q_t[lanes, :]
        fresh_k = kn_t[lanes, :]

        def score_group(group, inner):
            at_tok = tok_b - (group * 8).astype(F32).astype(BF16)
            rows = []
            for i in range(8):
                step = group * 8 + i
                keys = jnp.where(at_tok == jnp.asarray(i, BF16), fresh_k, k_buf[head, step])
                k_buf[head, step] = keys
                rows.append(jnp.sum(keys.astype(F32) * query, axis=0, keepdims=True))
            probs[pl.ds(pl.multiple_of(group * 8, 8), 8), :] = jnp.concatenate(rows, axis=0)
            return inner
        lax.fori_loop(0, T_LEN // 8, score_group, 0)
        out_copy(k_buf, nk, ko_sem, head).start()
        scores = probs[...] + bias[head]
        weights = jnp.exp(scores - jnp.max(scores, axis=0, keepdims=True))
        weights = weights / jnp.sum(weights, axis=0, keepdims=True)
        probs[...] = weights.astype(BF16).astype(F32)
        in_copy(sv, v_buf, v_sem, head).wait()
        fresh_v = vn_t[lanes, :]

        def mix_group(group, total):
            at_tok = tok_b - (group * 8).astype(F32).astype(BF16)
            for i in range(8):
                step = group * 8 + i
                vals = jnp.where(at_tok == jnp.asarray(i, BF16), fresh_v, v_buf[head, step])
                v_buf[head, step] = vals
                total = total + vals.astype(F32) * probs[pl.ds(step, 1), :]
            return total
        mix[lanes, :] = lax.fori_loop(0, T_LEN // 8, mix_group, jnp.zeros((HEAD_DIM, ROWS), F32))
        out_copy(v_buf, nv, vo_sem, head).start()
        return carry
    lax.fori_loop(0, HEADS, head_step, 0)

    mixed = jnp.concatenate([jnp.transpose(mix[block * 128:(block + 1) * 128, :]).astype(BF16)
                             for block in range(FLAT // 128)], axis=1)
    wo_copy.wait()

    def o_step(block, carry):
        cols = pl.ds(pl.multiple_of(block * 512, 512), 512)
        part_ref[:, cols] = jnp.dot(mixed, wo_buf[:, cols], preferred_element_type=F32).astype(BF16)
        return carry
    lax.fori_loop(0, D_MODEL // 512, o_step, 0)

    def end_out(head, carry):
        out_copy(k_buf, nk, ko_sem, head).wait()
        out_copy(v_buf, nv, vo_sem, head).wait()
        return carry
    lax.fori_loop(0, HEADS, end_out, 0)


def self_stage(x_in, tok_row, rel_t, norm_row, w_q, w_k, w_v, w_o, sk_t, sv_t):
    hbm = pl.BlockSpec(memory_space=pl.ANY)
    vmem = pl.BlockSpec(memory_space=pltpu.VMEM)
    cache = jax.ShapeDtypeStruct((T_LEN, HEADS, HEAD_DIM, ROWS), BF16)
    dma = pltpu.SemaphoreType.DMA
    return pl.pallas_call(
        self_kernel,
        out_shape=(jax.ShapeDtypeStruct((ROWS, D_MODEL), BF16), cache, cache),
        in_specs=[hbm, vmem, vmem, vmem] + [hbm] * 6,
        out_specs=(vmem, hbm, hbm),
        scratch_shapes=[
            pltpu.VMEM((ROWS, D_MODEL), BF16), pltpu.VMEM((ROWS, D_MODEL), BF16),
            pltpu.VMEM((D_MODEL, 3 * FLAT), BF16), pltpu.VMEM((FLAT, D_MODEL), BF16),
            pltpu.VMEM((HEADS, T_LEN, HEAD_DIM, ROWS), BF16), pltpu.VMEM((HEADS, T_LEN, HEAD_DIM, ROWS), BF16),
            pltpu.VMEM((ROWS, 3 * FLAT), F32), pltpu.VMEM((FLAT, ROWS), F32),
            pltpu.VMEM((FLAT, ROWS), BF16), pltpu.VMEM((FLAT, ROWS), BF16),
            pltpu.VMEM((HEADS, T_LEN, ROWS), F32), pltpu.VMEM((T_LEN, ROWS), F32), pltpu.VMEM((FLAT, ROWS), F32),
            dma, dma((N_CHUNK, 3)), dma, dma((HEADS,)), dma((HEADS,)), dma((HEADS,)), dma((HEADS,)),
        ],
        compiler_params=pltpu.CompilerParams(vmem_limit_bytes=56 * 1024 * 1024),
        cost_estimate=pl.CostEstimate(flops=10 ** 9, bytes_accessed=50 * 2 ** 20, transcendentals=0),
        name='self_stage',
    )(x_in, tok_row, rel_t, norm_row, w_q, w_k, w_v, w_o, sk_t, sv_t)


def project(normed, weight):
    return jnp.dot(normed, weight, preferred_element_type=F32).astype(BF16)


def attend(queries, keys_all, values_all, extra):
    scores = jnp.einsum('bhk,bthk->bht', queries, keys_all, preferred_element_type=jnp.float32) + extra
    probs_bf = jax.nn.softmax(scores, axis=-1).astype(jnp.bfloat16)
    mixed_out = jnp.einsum('bht,bthk->bhk', probs_bf, values_all, preferred_element_type=jnp.float32)
    return mixed_out.astype(jnp.bfloat16)


def solution(mesh):
    def tp_sum(partial_out):
        return lax.psum(partial_out.astype(jnp.bfloat16), 'tp').astype(jnp.float32)

    def local_layer(x_in, tok_pos, self_k, self_v, cross_k, cross_v, enc_mask, rel_bias, w_q, w_k, w_v, w_o, cross_q, cross_o, w_gate, w_up, w_down, norm_self, norm_cross, norm_mlp):
        head_shape = (ROWS, HEADS, HEAD_DIM)
        part, new_k, new_v = self_stage(
            x_in, tok_pos.reshape(1, ROWS), rel_bias.T, norm_self.reshape(1, D_MODEL), w_q, w_k, w_v, w_o,
            jnp.transpose(self_k, (1, 2, 3, 0)), jnp.transpose(self_v, (1, 2, 3, 0)))
        new_self_k = jnp.transpose(new_k, (3, 0, 1, 2))
        new_self_v = jnp.transpose(new_v, (3, 0, 1, 2))
        residual = x_in.astype(F32) + tp_sum(part)
        normed = rms_norm(residual, norm_cross.astype(F32))
        cross_queries = project(normed, cross_q).reshape(head_shape)
        cross_extra = jnp.where(enc_mask[:, None, :] != 0, 0.0, NEG_FILL)
        mixed_cross = attend(cross_queries, cross_k, cross_v, cross_extra)
        residual = residual + tp_sum(jnp.dot(mixed_cross.reshape(ROWS, FLAT), cross_o, preferred_element_type=jnp.float32))
        normed = rms_norm(residual, norm_mlp.astype(F32))
        gate_pre = jnp.dot(normed, w_gate, preferred_element_type=jnp.float32)
        up_pre = jnp.dot(normed, w_up, preferred_element_type=jnp.float32)
        hidden = (jax.nn.gelu(gate_pre, approximate=True) * up_pre).astype(jnp.bfloat16)
        residual = residual + tp_sum(jnp.dot(hidden, w_down, preferred_element_type=jnp.float32))
        return residual.astype(jnp.bfloat16), new_self_k, new_self_v

    cache_spec = P('dp', None, 'tp', None)
    split_cols = P(None, 'tp')
    split_rows = P('tp', None)
    in_specs = (P('dp', None), P('dp'), cache_spec, cache_spec, cache_spec, cache_spec, P('dp', None), P(None, 'tp'), split_cols, split_cols, split_cols, split_rows, split_cols, split_rows, split_cols, split_cols, split_rows, P(None), P(None), P(None))
    out_specs = (P('dp', None), cache_spec, cache_spec)
    return jax.shard_map(local_layer, mesh=mesh, in_specs=in_specs, out_specs=out_specs, check_vma=False)
```

time: 304 us -> 245 us (0.81)
  local copies, waits for them, and re-layouts: 38.5 us -> 2.32 us
  other arithmetic: 43.3 us -> 8.78 us
  Pallas kernels: 0 us -> 25.2 us
  matrix products: 58.7 us -> 45.6 us
    gather x1 -> x0, local copies, waits for them, and re-layouts: 27.7 us -> none  [self_terms(): jnp.take(rel_bias, rel_bucket(distance), axis=0)]
    pallas_call x0 -> x1, Pallas kernels: none -> 25.2 us  [self_stage(): pl.pallas_call(self_kernel, out_shape=(jax.ShapeDtypeStruct((ROWS, D_MODE...]
    dot_general x6 -> x2, matrix products: 20.3 us -> 7.18 us  [the longest x1 3.9 us: local_layer(): jnp.dot(mixed_cross.reshape(ROWS, FLAT), cross_o, preferred_element_type=...]
    unnamed x2 -> x0, other arithmetic: 11.6 us -> none
    dot_general x1 -> x0, other arithmetic: 11 us -> none  [attend(): jnp.einsum('bht,bthk->bhk', probs_bf, values_all, preferred_element_type=...]
    div x2 -> x1, other arithmetic: 7.25 us -> 0.38 us  [attend(): probs_bf = jax.nn.softmax(scores, axis=-1).astype(jnp.bfloat16)]
    unnamed x12 -> x10, local copies, waits for them, and re-layouts: 4.52 us -> 0.02 us
    dot_general x1 -> x0, local copies, waits for them, and re-layouts: 4.33 us -> none  [attend(): jnp.einsum('bhk,bthk->bht', queries, keys_all, preferred_element_type=jnp...]
where the time goes in v1:
time: 245 us; the launch traced here: 244 us
  waiting for transfers between devices  148 us (60%)
  matrix products  45.6 us (19%)
  Pallas kernels  25.2 us (10%)
  between operations  13.8 us (6%)
  other arithmetic  8.78 us (4%)
    psum x3, waiting for transfers between devices, tp_sum(): return lax.psum(partial_out.astype(jnp.bfloat16), 'tp').astype(jnp.float32)  148 us
    pallas_call x1, Pallas kernels, self_stage(): pl.pallas_call(self_kernel, out_shape=(jax.ShapeDtypeStruct((ROWS, D_MODE...  25.2 us
    dot_general x1, matrix products, attend(): jnp.einsum('bht,bthk->bhk', probs_bf, values_all, preferred_element_type=...  12.3 us
    dot_general x1, matrix products, local_layer(): jnp.dot(hidden, w_down, preferred_element_type=jnp.float32)  11.7 us
    dot_general x1, matrix products, attend(): jnp.einsum('bhk,bthk->bht', queries, keys_all, preferred_element_type=jnp...  8.04 us
    dot_general x1, matrix products, local_layer(): gate_pre = jnp.dot(normed, w_gate, preferred_element_type=jnp.float32)  6.37 us
  transfers between devices with their start and end apart: 3, of which 3 were waited for; matrix products, arithmetic and copies ran while one was open for 0% of the time, Pallas kernels for 0%

profile of v1, /device:TPU:0, one launch (start us, length us, event | category | flops | bytes accessed | tf_op | source)
XLA Modules:
  0.0 244.2 jit_solution(2045862906872192296)
XLA Ops:
  7.2 0.0 all-reduce.4.cloned.1.call-start
  7.2 1.3 reshape.42.norm_ref
  8.5 0.0 copy-start.3
  8.5 0.0 copy-start.2
  8.5 25.2 %self_stage.1 = (bf16[128,4096]{1,0:T(8,128)(2,1)}, bf16[64,8,64,128]{3,2,1,0:T(8,128)(2,1)}, bf16[64,8,64,128]{3,2,1,0:T(8,128)(2,1)}) custom-call(bf16[128,4096]{1,0:T(8,128)(2,1)} %x_hbm.1, s32[1,128]{1,0:T(1,128)} %bitcast.33, f32[8,32]{1,0:T(8,128)} %bitcast.32, bf16[1,4096]{1,0:T(2,128)(2,1)} %reshape.42.norm_ref, bf16[4096,512]{1,0:T(8,128)(2,1)} %wq.1, ...), custom_call_target="tpu_custom_call" | custom-call | flops 1000000000 | bytes 52428800 | tf_op jit(solution)/shard_map/self_stage/pallas_call | solution.py:171
  33.7 0.0 all-reduce.4.cloned.1.call-update
  33.7 0.0 all-reduce.6.cloned.1.call-start
  33.8 0.0 copy-done.3
  33.8 0.0 copy-done.2
  33.8 51.7 %all-reduce.4.cloned.1.call-done = bf16[128,4096]{1,0:T(8,128)(2,1)} async-done(((bf16[128,4096]{1,0:T(8,128)(2,1)}), bf16[128,4096]{1,0:T(8,128)(2,1)}) %all-reduce.4.cloned.1.call-update) | async-done | bytes 1048592 | tf_op jit(solution)/shard_map/psum | solution.py:204
  85.5 0.0 copy-done
  85.5 1.6 multiply_reduce_fusion.1
  87.2 3.3 %convolution_convert_fusion.2 = bf16[128,512]{1,0:T(8,128)(2,1)S(1)} fusion(bf16[4096,512]{1,0:T(8,128)(2,1)} %param.32, bf16[128,4096]{1,0:T(8,128)(2,1)} %all-reduce.4.cloned.1.call-done, bf16[128,4096]{1,0:T(8,128)(2,1)S(1)} %copy-done, f32[4096]{0:T(1024)S(1)} %convert_element_type.47, f32[128]{0:T(128)S(1)} %add_rsqrt_fusion.1), kind=kOutput, calls=%fused_computation.18 | convolution fusion | flops 540082176 | bytes 6439424 | tf_op jit(solution)/shard_map/dot_general | solution.py:192
  90.5 0.1 copy.24
  90.6 0.5 copy.25
  91.1 8.0 %fusion.31 = f32[128,8,1,128]{3,2,1,0:T(1,128)S(1)} fusion(bf16[128,8,64,1]{2,3,1,0:T(2,128)(2,1)S(1)} %copy.25, bf16[128,128,8,64]{1,3,2,0:T(8,128)(2,1)} %param.24), kind=kOutput, calls=%fused_computation.46 | convolution fusion | flops 16777216 | bytes 17432576 | tf_op jit(solution)/shard_map/bhk,bthk->bht/dot_general | solution.py:196
  99.1 0.4 fusion.7
  99.5 12.3 %fusion.17 = bf16[128,8,1,64]{3,2,1,0:T(2,128)(2,1)S(1)} fusion(bf16[128,128,8,64]{1,3,2,0:T(8,128)(2,1)} %param.25, bf16[128,8,128,1]{2,1,0,3:T(8,128)(2,1)S(1)} %fusion.7), kind=kOutput, calls=%fused_computation.29 | convolution fusion | flops 16777216 | bytes 17170432 | tf_op jit(solution)/shard_map/bht,bthk->bhk/dot_general | solution.py:198
  111.8 0.4 copy.28
  112.2 3.9 %convolution_convert_fusion.1 = bf16[128,4096]{1,0:T(8,128)(2,1)} fusion(bf16[128,512]{0,1:T(8,128)(2,1)S(1)} %bitcast.31, bf16[512,4096]{1,0:T(8,128)(2,1)} %param.33), kind=kOutput, calls=%fused_computation.3 | convolution fusion | flops 537395200 | bytes 5373952 | tf_op jit(solution)/shard_map/dot_general | solution.py:218
  116.1 0.0 all-reduce.6.cloned.1.call-update
  116.1 0.2 all-reduce.8.cloned.1.call-start
  116.3 0.0 copy-done.4
  116.4 48.1 %all-reduce.6.cloned.1.call-done = bf16[128,4096]{1,0:T(8,128)(2,1)} async-done(((bf16[128,4096]{1,0:T(8,128)(2,1)}), bf16[128,4096]{1,0:T(8,128)(2,1)}) %all-reduce.6.cloned.1.call-update) | async-done | bytes 1048592 | tf_op jit(solution)/shard_map/psum | solution.py:204
  164.4 0.0 copy-done.1
  164.4 1.8 multiply_reduce_fusion
  166.2 1.8 multiply_convert_fusion
  168.0 6.4 %fusion.32 = f32[128,1280]{1,0:T(8,128)} fusion(bf16[128,4096]{1,0:T(8,128)(2,1)S(1)} %multiply_convert_fusion, bf16[4096,1280]{1,0:T(8,128)(2,1)} %param.34), kind=kOutput, calls=%fused_computation.47 | convolution fusion | flops 1342177280 | bytes 12189696 | tf_op jit(solution)/shard_map/dot_general | solution.py:220
  174.4 11.7 %convolution_convert_fusion = bf16[128,4096]{1,0:T(8,128)(2,1)} fusion(bf16[1280,4096]{1,0:T(8,128)(2,1)} %param.36, bf16[128,4096]{1,0:T(8,128)(2,1)S(1)} %multiply_convert_fusion, bf16[4096,1280]{1,0:T(8,128)(2,1)} %param.35, f32[128,1280]{1,0:T(8,128)} %fusion.32), kind=kOutput, calls=%fused_computation.2 | convolution fusion | flops 2686517248 | bytes 23724032 | tf_op jit(solution)/shard_map/dot_general | solution.py:223
  186.1 0.0 all-reduce.8.cloned.1.call-update
  186.1 48.3 %all-reduce.8.cloned.1.call-done = bf16[128,4096]{1,0:T(8,128)(2,1)} async-done(((bf16[128,4096]{1,0:T(8,128)(2,1)}), bf16[128,4096]{1,0:T(8,128)(2,1)}) %all-reduce.8.cloned.1.call-update) | async-done | bytes 1048592 | tf_op jit(solution)/shard_map/psum | solution.py:204
  234.5 3.2 %add_convert_fusion = bf16[128,4096]{1,0:T(8,128)(2,1)} fusion(bf16[128,4096]{1,0:T(8,128)(2,1)} %all-reduce.8.cloned.1.call-done, bf16[128,4096]{1,0:T(8,128)(2,1)} %all-reduce.6.cloned.1.call-done, bf16[128,4096]{1,0:T(8,128)(2,1)S(1)} %copy-done.1, bf16[128,4096]{1,0:T(8,128)(2,1)S(1)} %copy-done), kind=kLoop, calls=%fused_computation.6 | loop fusion | flops 4194304 | bytes 5242880 | tf_op jit(solution)/shard_map/convert_element_type | solution.py:224
  (8 shorter events, 0.0 us)
Async XLA Ops:
  7.2 78.4 %all-reduce.4.cloned.1.call-start = ((), (), s32[]{:S(2)}) async-start(), calls=%async_computation | async-start | bytes 2097152 | tf_op jit(solution)/shard_map/psum | solution.py:204
  8.5 25.3 %copy-start.3 = (bf16[4096]{0:T(1024)(128)(2,1)S(1)}, bf16[4096]{0:T(1024)(128)(2,1)}, u32[]{:S(2)}) copy-start(bf16[4096]{0:T(1024)(128)(2,1)} %param.38) | copy-start | bytes 24580
  8.5 25.3 %copy-start.2 = (s32[128,128]{1,0:T(8,128)S(1)}, s32[128,128]{1,0:T(8,128)}, u32[]{:S(2)}) copy-start(s32[128,128]{1,0:T(8,128)} %param.26) | copy-start | bytes 196612
  8.5 77.0 %copy-start = (bf16[128,4096]{1,0:T(8,128)(2,1)S(1)}, bf16[128,4096]{1,0:T(8,128)(2,1)}, u32[]{:S(2)}) copy-start(bf16[128,4096]{1,0:T(8,128)(2,1)} %x_hbm.1) | copy-start | bytes 3145732
  33.7 130.7 %all-reduce.6.cloned.1.call-start = ((), (), s32[]{:S(2)}) async-start(), calls=%async_computation.1 | async-start | bytes 2097152 | tf_op jit(solution)/shard_map/psum | solution.py:204
  111.8 4.6 %copy-start.4 = (bf16[4096]{0:T(1024)(128)(2,1)S(1)}, bf16[4096]{0:T(1024)(128)(2,1)}, u32[]{:S(2)}) copy-start(bf16[4096]{0:T(1024)(128)(2,1)} %param.39) | copy-start | bytes 24580
  111.8 52.7 %copy-start.1 = (bf16[128,4096]{1,0:T(8,128)(2,1)S(1)}, bf16[128,4096]{1,0:T(8,128)(2,1)}, u32[]{:S(2)}) copy-start(bf16[128,4096]{1,0:T(8,128)(2,1)} %all-reduce.4.cloned.1.call-done) | copy-start | bytes 3145732
  116.1 118.4 %all-reduce.8.cloned.1.call-start = ((), (), s32[]{:S(2)}) async-start(), calls=%async_computation.2 | async-start | bytes 2097152 | tf_op jit(solution)/shard_map/psum | solution.py:204
Sparse Core Ops, SparseCore 0:
  33.8 51.6 all-reduce.3
  116.2 48.1 all-reduce.5
  186.3 48.1 all-reduce.7

commit v2 on v1

--- a/solution.py
+++ b/solution.py
@@ -152,7 +152,8 @@
 
     def o_step(block, carry):
         cols = pl.ds(pl.multiple_of(block * 512, 512), 512)
-        part_ref[:, cols] = jnp.dot(mixed, wo_buf[:, cols], preferred_element_type=F32).astype(BF16)
+        value = jnp.dot(mixed, wo_buf[:, cols], preferred_element_type=F32)
+        part_ref[:, :, cols] = value.reshape(16, 8, 512).astype(BF16)
         return carry
     lax.fori_loop(0, D_MODEL // 512, o_step, 0)
 
@@ -170,7 +171,7 @@
     dma = pltpu.SemaphoreType.DMA
     return pl.pallas_call(
         self_kernel,
-        out_shape=(jax.ShapeDtypeStruct((ROWS, D_MODEL), BF16), cache, cache),
+        out_shape=(jax.ShapeDtypeStruct((16, 8, D_MODEL), BF16), cache, cache),
         in_specs=[hbm, vmem, vmem, vmem] + [hbm] * 6,
         out_specs=(vmem, hbm, hbm),
         scratch_shapes=[
@@ -188,40 +189,318 @@
     )(x_in, tok_row, rel_t, norm_row, w_q, w_k, w_v, w_o, sk_t, sv_t)
 
 
-def project(normed, weight):
-    return jnp.dot(normed, weight, preferred_element_type=F32).astype(BF16)
-
-
-def attend(queries, keys_all, values_all, extra):
-    scores = jnp.einsum('bhk,bthk->bht', queries, keys_all, preferred_element_type=jnp.float32) + extra
-    probs_bf = jax.nn.softmax(scores, axis=-1).astype(jnp.bfloat16)
-    mixed_out = jnp.einsum('bht,bthk->bhk', probs_bf, values_all, preferred_element_type=jnp.float32)
-    return mixed_out.astype(jnp.bfloat16)
+GROUPS = 2
+GROUP_ROWS = ROWS // GROUPS
+OWN = GROUP_ROWS // 8
+STEP_ROWS = 8
+STEPS = ROWS // STEP_ROWS
+GROUP_STEPS = STEPS // GROUPS
+SLOTS = 9
+PAIR = 2 * HEADS
+MESH = pl.DeviceIdType.MESH
+
+
+def layer_kernel(part_in, x_hbm, enc_ref, nc_ref, nm_ref, ck, cv, wcq, wco, wg, wu, wd,
+                 out_ref,
+                 x_own, g_buf, u_buf, d_buf, co_buf, k_buf, v_buf, part, d2d_buf, chip_sum, rs_buf, h_full,
+                 h_rows, resid, q_buf, mixed, hidden, mask_buf,
+                 x_sem, cq_sem, co_sem, g_sem, u_sem, d_sem, k_sem, v_sem,
+                 dd_send, dd_recv, rs_send, rs_recv, ag_send, ag_recv, fw_send, fw_recv):
+    me = lax.axis_index('tp')
+    core = me % 2
+    chip = me // 2
+    partner = me + 1 - 2 * core
+    chips = (chip + 1 - 2 * (chip % 2), (chip + 2) % 4, 3 - chip)
+    peers = tuple(other * 2 + core for other in chips)
+
+    barrier = pltpu.get_barrier_semaphore()
+    for dev in (partner,) + peers:
+        pl.semaphore_signal(barrier, inc=1, device_id={'tp': dev}, device_id_type=MESH)
+
+    def block(group, half, which):
+        return group * 8 + half * 4 + which
+
+    x_copies = [pltpu.make_async_copy(x_hbm.at[block(g, core, chip)], x_own.at[g], x_sem.at[g]) for g in range(GROUPS)]
+    cq_copy = pltpu.make_async_copy(wcq, g_buf.at[:, pl.ds(0, FLAT)], cq_sem)
+    co_copy = pltpu.make_async_copy(wco, co_buf, co_sem)
+    g_copy = pltpu.make_async_copy(wg, g_buf, g_sem)
+    u_copy = pltpu.make_async_copy(wu, u_buf, u_sem)
+    d_copy = pltpu.make_async_copy(wd, d_buf, d_sem)
+    step_len = STEP_ROWS * FLAT
+
+    def kv_copies(step):
+        slot = step % SLOTS
+        span = pl.ds(pl.multiple_of(step * step_len, step_len), step_len)
+        return (pltpu.make_async_copy(ck.at[span, :], k_buf.at[slot], k_sem.at[slot]),
+                pltpu.make_async_copy(cv.at[span, :], v_buf.at[slot], v_sem.at[slot]))
+
+    def kv_start(step, carry=0):
+        for copy in kv_copies(step):
+            copy.start()
+        return carry
+
+    for copy in x_copies:
+        copy.start()
+    cq_copy.start()
+    lax.fori_loop(0, SLOTS, kv_start, 0)
+    co_copy.start()
+    u_copy.start()
+    d_copy.start()
+
+    mask_buf[...] = jnp.where(enc_ref[...] != 0, 0.0, NEG_FILL)
+    pl.semaphore_wait(barrier, 4)
+
+    def d2d(group, src):
+        return pltpu.make_async_remote_copy(
+            src_ref=src.at[pl.ds(block(group, 1 - core, 0), 4)], dst_ref=d2d_buf.at[group],
+            send_sem=dd_send.at[group], recv_sem=dd_recv.at[group], device_id={'tp': partner}, device_id_type=MESH)
+
+    def scatter(group, j):
+        return pltpu.make_async_remote_copy(
+            src_ref=chip_sum.at[group, chips[j]], dst_ref=rs_buf.at[group, j],
+            send_sem=rs_send.at[group, j], recv_sem=rs_recv.at[group, j],
+            device_id={'tp': peers[j]}, device_id_type=MESH)
+
+    def gather(group, j):
+        own = block(group, core, chip)
+        return pltpu.make_async_remote_copy(
+            src_ref=h_full.at[own], dst_ref=h_full.at[own],
+            send_sem=ag_send.at[group, j], recv_sem=ag_recv.at[group, j],
+            device_id={'tp': peers[j]}, device_id_type=MESH)
+
+    def forward(group, j):
+        piece = block(group, core, chip if j == 3 else chips[j])
+        return pltpu.make_async_remote_copy(
+            src_ref=h_full.at[piece], dst_ref=h_full.at[piece],
+            send_sem=fw_send.at[group, j], recv_sem=fw_recv.at[group, j],
+            device_id={'tp': partner}, device_id_type=MESH)
+
+    def reduce_chip(group, src):
+        d2d(group, src).wait()
+        for which in (3, 2, 1, 0):
+            total = (src[block(group, core, which)].astype(F32) + d2d_buf[group, which].astype(F32))
+            chip_sum[group, which] = total.astype(BF16)
+        for j in (2, 0, 1):
+            scatter(group, j).start()
+
+    def finish_rows(group, norm_row, last):
+        total = resid[group] + chip_sum[group, chip].astype(F32)
+        for j in range(3):
+            scatter(group, j).wait()
+            total = total + rs_buf[group, j].astype(F32)
+        resid[group] = total
+        own = block(group, core, chip)
+        h_full[own] = total.astype(BF16) if last else rms_norm(total, norm_row[...].astype(F32))
+        for j in (2, 0, 1):
+            gather(group, j).start()
+        forward(group, 3).start()
+
+    def pass_on(group):
+        for j in (0, 1, 2):
+            gather(group, j).wait()
+            forward(group, j).start()
+
+    def rows_ready(group):
+        for j in (3, 0, 1, 2):
+            forward(group, j).wait()
+
+    def collect(group):
+        rows_ready(group)
+
+        def two(i, carry):
+            pair = h_full[pl.ds(group * 8 + i * 2, 2)].astype(F32).reshape(16, D_MODEL)
+            h_rows[pl.ds(pl.multiple_of(group * GROUP_ROWS + i * 16, 16), 16), :] = pair.astype(BF16)
+            return carry
+        lax.fori_loop(0, GROUP_ROWS // 16, two, 0)
+
+    def out_product(group, left, weight_ref):
+        def cols_step(i, carry):
+            cols = pl.ds(pl.multiple_of(i * 512, 512), 512)
+            value = jnp.dot(left(), weight_ref[:, cols], preferred_element_type=F32)
+            part[pl.ds(group * 8, 8), :, cols] = value.reshape(8, OWN, 512).astype(BF16)
+            return carry
+        lax.fori_loop(0, D_MODEL // 512, cols_step, 0)
+
+    own_head = (lax.broadcasted_iota(jnp.int32, (HEADS, FLAT), 1) // HEAD_DIM
+                == lax.broadcasted_iota(jnp.int32, (HEADS, FLAT), 0))
+
+    def queries(group):
+        span = slice(group * GROUP_ROWS, (group + 1) * GROUP_ROWS)
+        value = jnp.dot(h_rows[span, :], g_buf[:, :FLAT], preferred_element_type=F32)
+        q_buf[span, :] = value.astype(BF16).astype(F32)
+
+    def cross_step(step):
+        slot = step % SLOTS
+        k_copy, v_copy = kv_copies(step)
+        k_copy.wait()
+        base = pl.multiple_of(step * STEP_ROWS, STEP_ROWS)
+        q_rows = q_buf[pl.ds(base, STEP_ROWS), :]
+        mask_rows = mask_buf[pl.ds(base, STEP_ROWS), :]
+        scores = []
+        for pair in range(STEP_ROWS // 2):
+            left = jnp.concatenate([jnp.where(own_head, q_rows[2 * pair + i:2 * pair + i + 1, :], 0.0) for i in range(2)], axis=0)
+            keys = jnp.concatenate([k_buf[slot, (2 * pair + i) * FLAT:(2 * pair + i + 1) * FLAT, :] for i in range(2)], axis=1)
+            both = jnp.dot(left.astype(BF16), keys, preferred_element_type=F32)
+            scores.append(both[:HEADS, :S_LEN] + mask_rows[2 * pair:2 * pair + 1, :])
+            scores.append(both[HEADS:, S_LEN:] + mask_rows[2 * pair + 1:2 * pair + 2, :])
+        score = jnp.concatenate(scores, axis=0)
+        weight = jnp.exp(score - jnp.max(score, axis=1, keepdims=True))
+        weight = weight / jnp.sum(weight, axis=1, keepdims=True)
+        v_copy.wait()
+        zeros = jnp.zeros((HEADS, S_LEN), F32)
+        rows = []
+        for pair in range(STEP_ROWS // 2):
+            first = weight[2 * pair * HEADS:(2 * pair + 1) * HEADS, :]
+            second = weight[(2 * pair + 1) * HEADS:(2 * pair + 2) * HEADS, :]
+            left = jnp.concatenate([jnp.concatenate([first, zeros], axis=1), jnp.concatenate([zeros, second], axis=1)], axis=0)
+            vals = jnp.concatenate([v_buf[slot, (2 * pair + i) * FLAT:(2 * pair + i + 1) * FLAT, :] for i in range(2)], axis=1)
+            both = lax.dot_general(left.astype(BF16), vals, (((1,), (1,)), ((), ())), preferred_element_type=F32)
+            for i in range(2):
+                mine = jnp.where(own_head, both[i * HEADS:(i + 1) * HEADS, :], 0.0)
+                rows.append(jnp.sum(mine, axis=0, keepdims=True))
+        mixed[pl.ds(base, STEP_ROWS), :] = jnp.concatenate(rows, axis=0)
+
+    def cross_out(group):
+        span = slice(group * GROUP_ROWS, (group + 1) * GROUP_ROWS)
+        out_product(group, lambda: mixed[span, :].astype(BF16), co_buf)
+
+    def mlp_in(group, at_block):
+        span = slice(group * GROUP_ROWS, (group + 1) * GROUP_ROWS)
+
+        def unit_step(i, carry):
+            at_block(i)
+            cols = pl.ds(pl.multiple_of(i * 256, 256), 256)
+            gate = jnp.dot(h_rows[span, :], g_buf[:, cols], preferred_element_type=F32)
+            up = jnp.dot(h_rows[span, :], u_buf[:, cols], preferred_element_type=F32)
+            hidden[:, cols] = (jax.nn.gelu(gate, approximate=True) * up).astype(BF16)
+            return carry
+        lax.fori_loop(0, UNITS // 256, unit_step, 0)
+
+    def mlp_out(group):
+        out_product(group, lambda: hidden[...], d_buf)
+
+    for g in range(GROUPS):
+        d2d(g, part_in).start()
+    for g in range(GROUPS):
+        reduce_chip(g, part_in)
+    for g in range(GROUPS):
+        x_copies[g].wait()
+        resid[g] = x_own[g].astype(F32)
+        finish_rows(g, nc_ref, False)
+    pass_on(0)
+    cq_copy.wait()
+    collect(0)
+    queries(0)
+
+    def first_group(i, carry):
+        @pl.when(i == 3)
+        def _():
+            pass_on(1)
+            collect(1)
+            queries(1)
+            g_copy.start()
+        cross_step(i)
+
+        @pl.when(i < STEPS - SLOTS)
+        def _():
+            kv_start(i + SLOTS)
+        return carry
+    lax.fori_loop(0, GROUP_STEPS, first_group, 0)
+    co_copy.wait()
+    cross_out(0)
+    d2d(0, part).start()
+
+    def second_group(i, carry):
+        @pl.when(i == 2)
+        def _():
+            reduce_chip(0, part)
+
+        @pl.when(i == 6)
+        def _():
+            finish_rows(0, nm_ref, False)
+        cross_step(i + GROUP_STEPS)
+        return carry
+    lax.fori_loop(0, GROUP_STEPS, second_group, 0)
+    cross_out(1)
+    d2d(1, part).start()
+    pass_on(0)
+    reduce_chip(1, part)
+    collect(0)
+    g_copy.wait()
+    u_copy.wait()
+    d_copy.wait()
+
+    def mid_first(i):
+        @pl.when(i == 3)
+        def _():
+            finish_rows(1, nm_ref, False)
+    mlp_in(0, mid_first)
+    mlp_out(0)
+    d2d(0, part).start()
+    pass_on(1)
+    collect(1)
+
+    def mid_second(i):
+        @pl.when(i == 1)
+        def _():
+            reduce_chip(0, part)
+    mlp_in(1, mid_second)
+    mlp_out(1)
+    d2d(1, part).start()
+    finish_rows(0, nm_ref, True)
+    reduce_chip(1, part)
+    pass_on(0)
+    finish_rows(1, nm_ref, True)
+    rows_ready(0)
+    out_ref[0:8] = h_full[0:8]
+    pass_on(1)
+    rows_ready(1)
+    out_ref[8:16] = h_full[8:16]
+
+
+def layer_stage(part, x_blocks, enc_mask, norm_cross, norm_mlp, ck, cv, cross_q, cross_o, w_gate, w_up, w_down):
+    hbm = pl.BlockSpec(memory_space=pl.ANY)
+    vmem = pl.BlockSpec(memory_space=pltpu.VMEM)
+    dma = pltpu.SemaphoreType.DMA
+    blocks = (2 * 8, OWN, D_MODEL)
+    return pl.pallas_call(
+        layer_kernel,
+        out_shape=jax.ShapeDtypeStruct(blocks, BF16),
+        in_specs=[vmem, hbm, vmem, vmem, vmem] + [hbm] * 7,
+        out_specs=vmem,
+        scratch_shapes=[
+            pltpu.VMEM((GROUPS, OWN, D_MODEL), BF16),
+            pltpu.VMEM((D_MODEL, UNITS), BF16), pltpu.VMEM((D_MODEL, UNITS), BF16), pltpu.VMEM((UNITS, D_MODEL), BF16),
+            pltpu.VMEM((FLAT, D_MODEL), BF16),
+            pltpu.VMEM((SLOTS, STEP_ROWS * FLAT, S_LEN), BF16), pltpu.VMEM((SLOTS, STEP_ROWS * FLAT, S_LEN), BF16),
+            pltpu.VMEM(blocks, BF16),
+            pltpu.VMEM((GROUPS, 4, OWN, D_MODEL), BF16), pltpu.VMEM((GROUPS, 4, OWN, D_MODEL), BF16),
+            pltpu.VMEM((GROUPS, 3, OWN, D_MODEL), BF16), pltpu.VMEM(blocks, BF16),
+            pltpu.VMEM((ROWS, D_MODEL), BF16), pltpu.VMEM((GROUPS, OWN, D_MODEL), F32),
+            pltpu.VMEM((ROWS, FLAT), F32), pltpu.VMEM((ROWS, FLAT), F32), pltpu.VMEM((GROUP_ROWS, UNITS), BF16),
+            pltpu.VMEM((ROWS, S_LEN), F32),
+            dma((GROUPS,)), dma, dma, dma, dma, dma, dma((SLOTS,)), dma((SLOTS,)),
+            dma((GROUPS,)), dma((GROUPS,)), dma((GROUPS, 3)), dma((GROUPS, 3)), dma((GROUPS, 3)), dma((GROUPS, 3)),
+            dma((GROUPS, 4)), dma((GROUPS, 4)),
+        ],
+        compiler_params=pltpu.CompilerParams(collective_id=0, has_side_effects=True, vmem_limit_bytes=67043328),
+        cost_estimate=pl.CostEstimate(flops=10 ** 10, bytes_accessed=70 * 2 ** 20, transcendentals=0),
+        name='layer_stage',
+    )(part, x_blocks, enc_mask, norm_cross, norm_mlp, ck, cv, cross_q, cross_o, w_gate, w_up, w_down)
 
 
 def solution(mesh):
-    def tp_sum(partial_out):
-        return lax.psum(partial_out.astype(jnp.bfloat16), 'tp').astype(jnp.float32)
-
     def local_layer(x_in, tok_pos, self_k, self_v, cross_k, cross_v, enc_mask, rel_bias, w_q, w_k, w_v, w_o, cross_q, cross_o, w_gate, w_up, w_down, norm_self, norm_cross, norm_mlp):
-        head_shape = (ROWS, HEADS, HEAD_DIM)
         part, new_k, new_v = self_stage(
             x_in, tok_pos.reshape(1, ROWS), rel_bias.T, norm_self.reshape(1, D_MODEL), w_q, w_k, w_v, w_o,
             jnp.transpose(self_k, (1, 2, 3, 0)), jnp.transpose(self_v, (1, 2, 3, 0)))
         new_self_k = jnp.transpose(new_k, (3, 0, 1, 2))
         new_self_v = jnp.transpose(new_v, (3, 0, 1, 2))
-        residual = x_in.astype(F32) + tp_sum(part)
-        normed = rms_norm(residual, norm_cross.astype(F32))
-        cross_queries = project(normed, cross_q).reshape(head_shape)
-        cross_extra = jnp.where(enc_mask[:, None, :] != 0, 0.0, NEG_FILL)
-        mixed_cross = attend(cross_queries, cross_k, cross_v, cross_extra)
-        residual = residual + tp_sum(jnp.dot(mixed_cross.reshape(ROWS, FLAT), cross_o, preferred_element_type=jnp.float32))
-        normed = rms_norm(residual, norm_mlp.astype(F32))
-        gate_pre = jnp.dot(normed, w_gate, preferred_element_type=jnp.float32)
-        up_pre = jnp.dot(normed, w_up, preferred_element_type=jnp.float32)
-        hidden = (jax.nn.gelu(gate_pre, approximate=True) * up_pre).astype(jnp.bfloat16)
-        residual = residual + tp_sum(jnp.dot(hidden, w_down, preferred_element_type=jnp.float32))
-        return residual.astype(jnp.bfloat16), new_self_k, new_self_v
+        ck = jnp.transpose(cross_k, (0, 2, 3, 1)).reshape(ROWS * FLAT, S_LEN)
+        cv = jnp.transpose(cross_v, (0, 2, 3, 1)).reshape(ROWS * FLAT, S_LEN)
+        out = layer_stage(part, x_in.reshape(2 * 8, OWN, D_MODEL), enc_mask, norm_cross.reshape(1, D_MODEL),
+                          norm_mlp.reshape(1, D_MODEL), ck, cv, cross_q, cross_o, w_gate, w_up, w_down)
+        return out.reshape(ROWS, D_MODEL), new_self_k, new_self_v
 
     cache_spec = P('dp', None, 'tp', None)
     split_cols = P(None, 'tp')

time: 245 us -> 104 us (0.42)
  waiting for transfers between devices: 148 us -> 0 us
  Pallas kernels: 25.2 us -> 97 us
  matrix products: 45.6 us -> 0 us
  between operations: 13.8 us -> 0.65 us
  other arithmetic: 8.78 us -> 0 us
  local copies, waits for them, and re-layouts: 2.32 us -> 6.2 us
    psum x3 -> x0, waiting for transfers between devices: 148 us -> none  [tp_sum(): return lax.psum(partial_out.astype(jnp.bfloat16), 'tp').astype(jnp.float32)]
    pallas_call x1 -> x2, Pallas kernels: 25.2 us -> 97 us  [the longest x1 75.6 us: layer_stage(): pl.pallas_call(layer_kernel, out_shape=jax.ShapeDtypeStruct(blocks, BF16)...]
    dot_general x6 -> x0, matrix products: 45.6 us -> none  [the longest x1 12.3 us: attend(): jnp.einsum('bht,bthk->bhk', probs_bf, values_all, preferred_element_type=...]
    convert_element_type x4 -> x0, other arithmetic: 4.96 us -> none  [the longest x1 3.17 us: local_layer(): return (residual.astype(jnp.bfloat16), new_self_k, new_self_v)]
    reduce_sum x2 -> x0, other arithmetic: 3.42 us -> none  [rms_norm(): jnp.mean(values * values, axis=-1, keepdims=True) + 1e-06]
  transfers between devices with their start and end apart: 3 -> 0, of which waited for: 3 -> 0; matrix products, arithmetic and copies ran while one was open for 0% -> 0% of each run, Pallas kernels for 0% -> 0%
where the time goes in v2:
time: 104 us
  Pallas kernels  97 us (93%)
  local copies, waits for them, and re-layouts  6.2 us (6%)
    pallas_call x1, Pallas kernels, layer_stage(): pl.pallas_call(layer_kernel, out_shape=jax.ShapeDtypeStruct(blocks, BF16)...  75.6 us
    pallas_call x1, Pallas kernels, self_stage(): pl.pallas_call(self_kernel, out_shape=(jax.ShapeDtypeStruct((16, 8, D_MOD...  21.4 us
    unnamed x1, local copies, waits for them, and re-layouts  2.29 us

profile of v2, /device:TPU:0, one launch (start us, length us, event | category | flops | bytes accessed | tf_op | source)
XLA Modules:
  0.0 103.8 jit_solution(7365895226786760674)
XLA Ops:
  0.6 1.3 %reshape.31.norm_ref = bf16[1,4096]{1,0:T(2,128)(2,1)} reshape(bf16[4096]{0:T(1024)(128)(2,1)} %param.37) | data formatting | bytes 16384 | tf_op jit(solution)/shard_map/reshape | solution.py:495
  1.9 1.3 %reshape.33.nc_ref = bf16[1,4096]{1,0:T(2,128)(2,1)} reshape(bf16[4096]{0:T(1024)(128)(2,1)} %param.38) | data formatting | bytes 16384 | tf_op jit(solution)/shard_map/reshape | solution.py:501
  3.2 1.3 %reshape.34.nm_ref = bf16[1,4096]{1,0:T(2,128)(2,1)} reshape(bf16[4096]{0:T(1024)(128)(2,1)} %param.39) | data formatting | bytes 16384 | tf_op jit(solution)/shard_map/reshape | solution.py:502
  4.5 21.4 %self_stage.1 = (bf16[16,8,4096]{2,1,0:T(8,128)(2,1)}, bf16[64,8,64,128]{3,2,1,0:T(8,128)(2,1)}, bf16[64,8,64,128]{3,2,1,0:T(8,128)(2,1)}) custom-call(bf16[128,4096]{1,0:T(8,128)(2,1)} %x_hbm.1, s32[1,128]{1,0:T(1,128)} %bitcast.21, f32[8,32]{1,0:T(8,128)} %bitcast.20, bf16[1,4096]{1,0:T(2,128)(2,1)} %reshape.31.norm_ref, bf16[4096,512]{1,0:T(8,128)(2,1)} %wq.1, ...), custom_call_target="tpu_custom_call" | custom-call | flops 1000000000 | bytes 52428800 | tf_op jit(solution)/shard_map/self_stage/pallas_call | solution.py:172
  25.9 75.6 %layer_stage.1 = bf16[16,8,4096]{2,1,0:T(8,128)(2,1)} custom-call(bf16[16,8,4096]{2,1,0:T(8,128)(2,1)} %get-tuple-element.6.part_in, bf16[16,8,4096]{2,1,0:T(8,128)(2,1)} %bitcast.18, s32[128,128]{1,0:T(8,128)} %enc_ref.1, bf16[1,4096]{1,0:T(2,128)(2,1)} %reshape.33.nc_ref, bf16[1,4096]{1,0:T(2,128)(2,1)} %reshape.34.nm_ref, bf16[65536,128]{1,0:T(8,128)(2,1)} %bitcast.14, ...), custom_call_target="tpu_custom_call" | custom-call | flops 10000000000 | bytes 73400320 | tf_op jit(solution)/shard_map/layer_stage/pallas_call | solution.py:466
  101.6 2.3 %copy.24 = bf16[128,4096]{1,0:T(8,128)(2,1)} copy(bf16[128,4096]{1,0:T(8,128)(2,1)} %bitcast.19) | data formatting | bytes 2097152

commit v3 on v2

--- a/solution.py
+++ b/solution.py
@@ -20,6 +20,11 @@
 def rms_norm(values, norm_scale):
     inv_rms = lax.rsqrt(jnp.mean(values * values, axis=-1, keepdims=True) + 1e-6)
     return (values * inv_rms * norm_scale).astype(BF16)
+
+
+def lane_row(blocks):
+    rows = blocks.astype(F32)
+    return jnp.concatenate([rows[i:i + 1, :] for i in range(rows.shape[0])], axis=1)
 
 
 def bias_table(rel_bias_t, tok_row):
@@ -48,7 +53,7 @@
 
 def self_kernel(x_hbm, tok_ref, rel_ref, norm_ref, wq, wk, wv, wo, sk, sv,
                 part_ref, nk, nv,
-                x_buf, h_buf, w_buf, wo_buf, k_buf, v_buf, acc, q_t, kn_t, vn_t, bias, probs, mix,
+                x_buf, h_buf, w_buf, wo_buf, k_buf, v_buf, acc, q_t, kn_t, vn_t, bias, probs, mix, norm_row,
                 x_sem, w_sem, wo_sem, k_sem, v_sem, ko_sem, vo_sem):
     x_copy = pltpu.make_async_copy(x_hbm, x_buf, x_sem)
     x_copy.start()
@@ -81,11 +86,12 @@
     for head, table in enumerate(bias_table(rel_ref[...], tok_row)):
         bias[head] = table
 
+    norm_row[...] = lane_row(norm_ref[...])
     x_copy.wait()
 
     def norm_rows(step, carry):
         rows = pl.ds(pl.multiple_of(step * 16, 16), 16)
-        h_buf[rows, :] = rms_norm(x_buf[rows, :].astype(F32), norm_ref[...].astype(F32))
+        h_buf[rows, :] = rms_norm(x_buf[rows, :].astype(F32), norm_row[...])
         return carry
     lax.fori_loop(0, ROWS // 16, norm_rows, 0)
 
@@ -107,6 +113,11 @@
             dst[block * 128:(block + 1) * 128, :] = turned.astype(BF16).astype(dst.dtype)
 
     tok_b = jnp.broadcast_to(tok_row.astype(F32), (HEAD_DIM, ROWS)).astype(BF16)
+
+    def start_out(head, carry):
+        out_copy(k_buf, nk, ko_sem, head).start()
+        out_copy(v_buf, nv, vo_sem, head).start()
+        return carry
 
     def head_step(head, carry):
         lanes = pl.ds(pl.multiple_of(head * HEAD_DIM, HEAD_DIM), HEAD_DIM)
@@ -125,7 +136,6 @@
             probs[pl.ds(pl.multiple_of(group * 8, 8), 8), :] = jnp.concatenate(rows, axis=0)
             return inner
         lax.fori_loop(0, T_LEN // 8, score_group, 0)
-        out_copy(k_buf, nk, ko_sem, head).start()
         scores = probs[...] + bias[head]
         weights = jnp.exp(scores - jnp.max(scores, axis=0, keepdims=True))
         weights = weights / jnp.sum(weights, axis=0, keepdims=True)
@@ -142,7 +152,8 @@
                 total = total + vals.astype(F32) * probs[pl.ds(step, 1), :]
             return total
         mix[lanes, :] = lax.fori_loop(0, T_LEN // 8, mix_group, jnp.zeros((HEAD_DIM, ROWS), F32))
-        out_copy(v_buf, nv, vo_sem, head).start()
+
+        start_out(head, 0)
         return carry
     lax.fori_loop(0, HEADS, head_step, 0)
 
@@ -150,12 +161,9 @@
                              for block in range(FLAT // 128)], axis=1)
     wo_copy.wait()
 
-    def o_step(block, carry):
-        cols = pl.ds(pl.multiple_of(block * 512, 512), 512)
-        value = jnp.dot(mixed, wo_buf[:, cols], preferred_element_type=F32)
-        part_ref[:, :, cols] = value.reshape(16, 8, 512).astype(BF16)
-        return carry
-    lax.fori_loop(0, D_MODEL // 512, o_step, 0)
+    for start in range(0, D_MODEL, 1024):
+        value = jnp.dot(mixed, wo_buf[:, start:start + 1024], preferred_element_type=F32)
+        part_ref[:, :, start:start + 1024] = value.reshape(16, 8, 1024).astype(BF16)
 
     def end_out(head, carry):
         out_copy(k_buf, nk, ko_sem, head).wait()
@@ -165,7 +173,7 @@
 
 
 def self_stage(x_in, tok_row, rel_t, norm_row, w_q, w_k, w_v, w_o, sk_t, sv_t):
-    hbm = pl.BlockSpec(memory_space=pl.ANY)
+    hbm = pl.BlockSpec(memory_space=pltpu.HBM)
     vmem = pl.BlockSpec(memory_space=pltpu.VMEM)
     cache = jax.ShapeDtypeStruct((T_LEN, HEADS, HEAD_DIM, ROWS), BF16)
     dma = pltpu.SemaphoreType.DMA
@@ -181,9 +189,10 @@
             pltpu.VMEM((ROWS, 3 * FLAT), F32), pltpu.VMEM((FLAT, ROWS), F32),
             pltpu.VMEM((FLAT, ROWS), BF16), pltpu.VMEM((FLAT, ROWS), BF16),
             pltpu.VMEM((HEADS, T_LEN, ROWS), F32), pltpu.VMEM((T_LEN, ROWS), F32), pltpu.VMEM((FLAT, ROWS), F32),
+            pltpu.VMEM((1, D_MODEL), F32),
             dma, dma((N_CHUNK, 3)), dma, dma((HEADS,)), dma((HEADS,)), dma((HEADS,)), dma((HEADS,)),
         ],
-        compiler_params=pltpu.CompilerParams(vmem_limit_bytes=56 * 1024 * 1024),
+        compiler_params=pltpu.CompilerParams(vmem_limit_bytes=60 * 1024 * 1024),
         cost_estimate=pl.CostEstimate(flops=10 ** 9, bytes_accessed=50 * 2 ** 20, transcendentals=0),
         name='self_stage',
     )(x_in, tok_row, rel_t, norm_row, w_q, w_k, w_v, w_o, sk_t, sv_t)
@@ -192,10 +201,12 @@
 GROUPS = 2
 GROUP_ROWS = ROWS // GROUPS
 OWN = GROUP_ROWS // 8
-STEP_ROWS = 8
+STEP_ROWS = 16
+SPLIT = 2
+OUT_COLS = D_MODEL // SPLIT
 STEPS = ROWS // STEP_ROWS
 GROUP_STEPS = STEPS // GROUPS
-SLOTS = 9
+SLOTS = 4
 PAIR = 2 * HEADS
 MESH = pl.DeviceIdType.MESH
 
@@ -203,7 +214,7 @@
 def layer_kernel(part_in, x_hbm, enc_ref, nc_ref, nm_ref, ck, cv, wcq, wco, wg, wu, wd,
                  out_ref,
                  x_own, g_buf, u_buf, d_buf, co_buf, k_buf, v_buf, part, d2d_buf, chip_sum, rs_buf, h_full,
-                 h_rows, resid, q_buf, mixed, hidden, mask_buf,
+                 h_rows, resid, q_buf, mixed, hidden, mask_buf, norm_rows,
                  x_sem, cq_sem, co_sem, g_sem, u_sem, d_sem, k_sem, v_sem,
                  dd_send, dd_recv, rs_send, rs_recv, ag_send, ag_recv, fw_send, fw_recv):
     me = lax.axis_index('tp')
@@ -247,62 +258,78 @@
     u_copy.start()
     d_copy.start()
 
+    norm_rows[0] = lane_row(nc_ref[...])
+    norm_rows[1] = lane_row(nm_ref[...])
     mask_buf[...] = jnp.where(enc_ref[...] != 0, 0.0, NEG_FILL)
     pl.semaphore_wait(barrier, 4)
 
-    def d2d(group, src):
+    def columns(part_no):
+        return pl.ds(part_no * OUT_COLS, OUT_COLS)
+
+    def d2d(group, src, part_no):
         return pltpu.make_async_remote_copy(
-            src_ref=src.at[pl.ds(block(group, 1 - core, 0), 4)], dst_ref=d2d_buf.at[group],
-            send_sem=dd_send.at[group], recv_sem=dd_recv.at[group], device_id={'tp': partner}, device_id_type=MESH)
-
-    def scatter(group, j):
+            src_ref=src.at[pl.ds(block(group, 1 - core, 0), 4), :, columns(part_no)],
+            dst_ref=d2d_buf.at[group, :, :, columns(part_no)],
+            send_sem=dd_send.at[group, part_no], recv_sem=dd_recv.at[group, part_no],
+            device_id={'tp': partner}, device_id_type=MESH)
+
+    def scatter(group, j, part_no):
         return pltpu.make_async_remote_copy(
-            src_ref=chip_sum.at[group, chips[j]], dst_ref=rs_buf.at[group, j],
-            send_sem=rs_send.at[group, j], recv_sem=rs_recv.at[group, j],
+            src_ref=chip_sum.at[group, chips[j], :, columns(part_no)], dst_ref=rs_buf.at[group, j, :, columns(part_no)],
+            send_sem=rs_send.at[group, j, part_no], recv_sem=rs_recv.at[group, j, part_no],
             device_id={'tp': peers[j]}, device_id_type=MESH)
 
-    def gather(group, j):
+    def gather(group, j, rows_ref):
         own = block(group, core, chip)
         return pltpu.make_async_remote_copy(
-            src_ref=h_full.at[own], dst_ref=h_full.at[own],
+            src_ref=rows_ref.at[own], dst_ref=rows_ref.at[own],
             send_sem=ag_send.at[group, j], recv_sem=ag_recv.at[group, j],
             device_id={'tp': peers[j]}, device_id_type=MESH)
 
-    def forward(group, j):
+    def forward(group, j, rows_ref):
         piece = block(group, core, chip if j == 3 else chips[j])
         return pltpu.make_async_remote_copy(
-            src_ref=h_full.at[piece], dst_ref=h_full.at[piece],
+            src_ref=rows_ref.at[piece], dst_ref=rows_ref.at[piece],
             send_sem=fw_send.at[group, j], recv_sem=fw_recv.at[group, j],
             device_id={'tp': partner}, device_id_type=MESH)
 
+    def d2d_start(group, src):
+        for part_no in range(SPLIT):
+            d2d(group, src, part_no).start()
+
     def reduce_chip(group, src):
-        d2d(group, src).wait()
-        for which in (3, 2, 1, 0):
-            total = (src[block(group, core, which)].astype(F32) + d2d_buf[group, which].astype(F32))
-            chip_sum[group, which] = total.astype(BF16)
+        for part_no in range(SPLIT):
+            d2d(group, src, part_no).wait()
+            cols = columns(part_no)
+            for which in range(4):
+                total = src[block(group, core, which), :, cols].astype(F32) + d2d_buf[group, which, :, cols].astype(F32)
+                chip_sum[group, which, :, cols] = total.astype(BF16)
+            for j in (2, 0, 1):
+                scatter(group, j, part_no).start()
+
+    def finish_rows(group, norm, last):
+        for part_no in range(SPLIT):
+            cols = columns(part_no)
+            total = resid[group, :, cols] + chip_sum[group, chip, :, cols].astype(F32)
+            for j in range(3):
+                scatter(group, j, part_no).wait()
+                total = total + rs_buf[group, j, :, cols].astype(F32)
+            resid[group, :, cols] = total
+        own = block(group, core, chip)
+        rows_ref = out_ref if last else h_full
+        rows_ref[own] = resid[group].astype(BF16) if last else rms_norm(resid[group], norm_rows[norm])
         for j in (2, 0, 1):
-            scatter(group, j).start()
-
-    def finish_rows(group, norm_row, last):
-        total = resid[group] + chip_sum[group, chip].astype(F32)
-        for j in range(3):
-            scatter(group, j).wait()
-            total = total + rs_buf[group, j].astype(F32)
-        resid[group] = total
-        own = block(group, core, chip)
-        h_full[own] = total.astype(BF16) if last else rms_norm(total, norm_row[...].astype(F32))
-        for j in (2, 0, 1):
-            gather(group, j).start()
-        forward(group, 3).start()
-
-    def pass_on(group):
+            gather(group, j, rows_ref).start()
+        forward(group, 3, rows_ref).start()
+
+    def pass_on(group, rows_ref=h_full):
         for j in (0, 1, 2):
-            gather(group, j).wait()
-            forward(group, j).start()
-
-    def rows_ready(group):
+            gather(group, j, rows_ref).wait()
+            forward(group, j, rows_ref).start()
+
+    def rows_ready(group, rows_ref=h_full):
         for j in (3, 0, 1, 2):
-            forward(group, j).wait()
+            forward(group, j, rows_ref).wait()
 
     def collect(group):
         rows_ready(group)
@@ -314,12 +341,12 @@
         lax.fori_loop(0, GROUP_ROWS // 16, two, 0)
 
     def out_product(group, left, weight_ref):
-        def cols_step(i, carry):
-            cols = pl.ds(pl.multiple_of(i * 512, 512), 512)
-            value = jnp.dot(left(), weight_ref[:, cols], preferred_element_type=F32)
-            part[pl.ds(group * 8, 8), :, cols] = value.reshape(8, OWN, 512).astype(BF16)
-            return carry
-        lax.fori_loop(0, D_MODEL // 512, cols_step, 0)
+        rows = left()
+        for part_no in range(SPLIT):
+            cols = slice(part_no * OUT_COLS, (part_no + 1) * OUT_COLS)
+            value = jnp.dot(rows, weight_ref[:, cols], preferred_element_type=F32)
+            part[group * 8:(group + 1) * 8, :, cols] = value.reshape(8, OWN, OUT_COLS).astype(BF16)
+            d2d(group, part, part_no).start()
 
     own_head = (lax.broadcasted_iota(jnp.int32, (HEADS, FLAT), 1) // HEAD_DIM
                 == lax.broadcasted_iota(jnp.int32, (HEADS, FLAT), 0))
@@ -380,64 +407,57 @@
         out_product(group, lambda: hidden[...], d_buf)
 
     for g in range(GROUPS):
-        d2d(g, part_in).start()
+        d2d_start(g, part_in)
     for g in range(GROUPS):
         reduce_chip(g, part_in)
     for g in range(GROUPS):
         x_copies[g].wait()
         resid[g] = x_own[g].astype(F32)
-        finish_rows(g, nc_ref, False)
+        finish_rows(g, 0, False)
     pass_on(0)
     cq_copy.wait()
     collect(0)
     queries(0)
 
     def first_group(i, carry):
-        @pl.when(i == 3)
-        def _():
-            pass_on(1)
-            collect(1)
-            queries(1)
-            g_copy.start()
         cross_step(i)
 
         @pl.when(i < STEPS - SLOTS)
         def _():
             kv_start(i + SLOTS)
         return carry
-    lax.fori_loop(0, GROUP_STEPS, first_group, 0)
+    lax.fori_loop(0, 3, first_group, 0)
+    pass_on(1)
+    lax.fori_loop(3, GROUP_STEPS, first_group, 0)
     co_copy.wait()
     cross_out(0)
-    d2d(0, part).start()
+    collect(1)
+    queries(1)
+    g_copy.start()
 
     def second_group(i, carry):
-        @pl.when(i == 2)
+        @pl.when(i == 1)
         def _():
             reduce_chip(0, part)
-
-        @pl.when(i == 6)
-        def _():
-            finish_rows(0, nm_ref, False)
         cross_step(i + GROUP_STEPS)
         return carry
     lax.fori_loop(0, GROUP_STEPS, second_group, 0)
     cross_out(1)
-    d2d(1, part).start()
+    finish_rows(0, 1, False)
+    reduce_chip(1, part)
     pass_on(0)
-    reduce_chip(1, part)
     collect(0)
     g_copy.wait()
     u_copy.wait()
     d_copy.wait()
 
     def mid_first(i):
-        @pl.when(i == 3)
+        @pl.when(i == 0)
         def _():
-            finish_rows(1, nm_ref, False)
+            finish_rows(1, 1, False)
     mlp_in(0, mid_first)
+    pass_on(1)
     mlp_out(0)
-    d2d(0, part).start()
-    pass_on(1)
     collect(1)
 
     def mid_second(i):
@@ -445,21 +465,18 @@
         def _():
             reduce_chip(0, part)
     mlp_in(1, mid_second)
+    finish_rows(0, 1, True)
     mlp_out(1)
-    d2d(1, part).start()
-    finish_rows(0, nm_ref, True)
     reduce_chip(1, part)
-    pass_on(0)
-    finish_rows(1, nm_ref, True)
-    rows_ready(0)
-    out_ref[0:8] = h_full[0:8]
-    pass_on(1)
-    rows_ready(1)
-    out_ref[8:16] = h_full[8:16]
+    pass_on(0, out_ref)
+    finish_rows(1, 1, True)
+    rows_ready(0, out_ref)
+    pass_on(1, out_ref)
+    rows_ready(1, out_ref)
 
 
 def layer_stage(part, x_blocks, enc_mask, norm_cross, norm_mlp, ck, cv, cross_q, cross_o, w_gate, w_up, w_down):
-    hbm = pl.BlockSpec(memory_space=pl.ANY)
+    hbm = pl.BlockSpec(memory_space=pltpu.HBM)
     vmem = pl.BlockSpec(memory_space=pltpu.VMEM)
     dma = pltpu.SemaphoreType.DMA
     blocks = (2 * 8, OWN, D_MODEL)
@@ -478,12 +495,13 @@
             pltpu.VMEM((GROUPS, 3, OWN, D_MODEL), BF16), pltpu.VMEM(blocks, BF16),
             pltpu.VMEM((ROWS, D_MODEL), BF16), pltpu.VMEM((GROUPS, OWN, D_MODEL), F32),
             pltpu.VMEM((ROWS, FLAT), F32), pltpu.VMEM((ROWS, FLAT), F32), pltpu.VMEM((GROUP_ROWS, UNITS), BF16),
-            pltpu.VMEM((ROWS, S_LEN), F32),
+            pltpu.VMEM((ROWS, S_LEN), F32), pltpu.VMEM((2, 1, D_MODEL), F32),
             dma((GROUPS,)), dma, dma, dma, dma, dma, dma((SLOTS,)), dma((SLOTS,)),
-            dma((GROUPS,)), dma((GROUPS,)), dma((GROUPS, 3)), dma((GROUPS, 3)), dma((GROUPS, 3)), dma((GROUPS, 3)),
+            dma((GROUPS, SPLIT)), dma((GROUPS, SPLIT)), dma((GROUPS, 3, SPLIT)), dma((GROUPS, 3, SPLIT)),
+            dma((GROUPS, 3)), dma((GROUPS, 3)),
             dma((GROUPS, 4)), dma((GROUPS, 4)),
         ],
-        compiler_params=pltpu.CompilerParams(collective_id=0, has_side_effects=True, vmem_limit_bytes=67043328),
+        compiler_params=pltpu.CompilerParams(collective_id=0, has_side_effects=True, vmem_limit_bytes=59 * 1024 * 1024),
         cost_estimate=pl.CostEstimate(flops=10 ** 10, bytes_accessed=70 * 2 ** 20, transcendentals=0),
         name='layer_stage',
     )(part, x_blocks, enc_mask, norm_cross, norm_mlp, ck, cv, cross_q, cross_o, w_gate, w_up, w_down)
@@ -492,14 +510,14 @@
 def solution(mesh):
     def local_layer(x_in, tok_pos, self_k, self_v, cross_k, cross_v, enc_mask, rel_bias, w_q, w_k, w_v, w_o, cross_q, cross_o, w_gate, w_up, w_down, norm_self, norm_cross, norm_mlp):
         part, new_k, new_v = self_stage(
-            x_in, tok_pos.reshape(1, ROWS), rel_bias.T, norm_self.reshape(1, D_MODEL), w_q, w_k, w_v, w_o,
+            x_in, tok_pos.reshape(1, ROWS), rel_bias.T, norm_self.reshape(32, 128), w_q, w_k, w_v, w_o,
             jnp.transpose(self_k, (1, 2, 3, 0)), jnp.transpose(self_v, (1, 2, 3, 0)))
         new_self_k = jnp.transpose(new_k, (3, 0, 1, 2))
         new_self_v = jnp.transpose(new_v, (3, 0, 1, 2))
         ck = jnp.transpose(cross_k, (0, 2, 3, 1)).reshape(ROWS * FLAT, S_LEN)
         cv = jnp.transpose(cross_v, (0, 2, 3, 1)).reshape(ROWS * FLAT, S_LEN)
-        out = layer_stage(part, x_in.reshape(2 * 8, OWN, D_MODEL), enc_mask, norm_cross.reshape(1, D_MODEL),
-                          norm_mlp.reshape(1, D_MODEL), ck, cv, cross_q, cross_o, w_gate, w_up, w_down)
+        out = layer_stage(part, x_in.reshape(2 * 8, OWN, D_MODEL), enc_mask, norm_cross.reshape(32, 128),
+                          norm_mlp.reshape(32, 128), ck, cv, cross_q, cross_o, w_gate, w_up, w_down)
         return out.reshape(ROWS, D_MODEL), new_self_k, new_self_v
 
     cache_spec = P('dp', None, 'tp', None)

time: 104 us -> 90.9 us (0.87)
  Pallas kernels: 97 us -> 87.8 us
  local copies, waits for them, and re-layouts: 6.2 us -> 2.29 us
    pallas_call x1, Pallas kernels: 75.6 us -> 67.2 us  [layer_stage(): pl.pallas_call(layer_kernel, out_shape=jax.ShapeDtypeStruct(blocks, BF16)...]
    reshape x3 -> x0, local copies, waits for them, and re-layouts: 3.91 us -> none  [the longest x1 1.31 us: local_layer(): norm_self.reshape(1, D_MODEL)]
where the time goes in v3:
time: 90.9 us; the launch traced here: 90.7 us
  Pallas kernels  87.8 us (97%)
  local copies, waits for them, and re-layouts  2.29 us (3%)
    pallas_call x1, Pallas kernels, layer_stage(): pl.pallas_call(layer_kernel, out_shape=jax.ShapeDtypeStruct(blocks, BF16)...  67.2 us
    pallas_call x1, Pallas kernels, self_stage(): pl.pallas_call(self_kernel, out_shape=(jax.ShapeDtypeStruct((16, 8, D_MOD...  20.6 us
    unnamed x1, local copies, waits for them, and re-layouts  2.29 us

profile of v3, /device:TPU:0, one launch (start us, length us, event | category | flops | bytes accessed | tf_op | source)
XLA Modules:
  0.0 90.7 jit_solution(16815119949384425975)
XLA Ops:
  0.6 20.6 %self_stage.1 = (bf16[16,8,4096]{2,1,0:T(8,128)(2,1)}, bf16[64,8,64,128]{3,2,1,0:T(8,128)(2,1)}, bf16[64,8,64,128]{3,2,1,0:T(8,128)(2,1)}) custom-call(bf16[128,4096]{1,0:T(8,128)(2,1)} %x_hbm.1, s32[1,128]{1,0:T(1,128)} %bitcast.27, f32[8,32]{1,0:T(8,128)} %bitcast.26, bf16[32,128]{1,0:T(8,128)(2,1)} %bitcast.25, bf16[4096,512]{1,0:T(8,128)(2,1)} %wq.1, ...), custom_call_target="tpu_custom_call" | custom-call | flops 1000000000 | bytes 52428800 | tf_op jit(solution)/shard_map/self_stage/pallas_call | solution.py:180
  21.2 67.2 %layer_stage.1 = bf16[16,8,4096]{2,1,0:T(8,128)(2,1)} custom-call(bf16[16,8,4096]{2,1,0:T(8,128)(2,1)} %get-tuple-element.6.part_in, bf16[16,8,4096]{2,1,0:T(8,128)(2,1)} %bitcast.21, s32[128,128]{1,0:T(8,128)} %enc_ref.1, bf16[32,128]{1,0:T(8,128)(2,1)} %bitcast.23, bf16[32,128]{1,0:T(8,128)(2,1)} %bitcast.24, bf16[65536,128]{1,0:T(8,128)(2,1)} %bitcast.17, ...), custom_call_target="tpu_custom_call" | custom-call | flops 10000000000 | bytes 73400320 | tf_op jit(solution)/shard_map/layer_stage/pallas_call | solution.py:483
  88.4 2.3 %copy.24 = bf16[128,4096]{1,0:T(8,128)(2,1)} copy(bf16[128,4096]{1,0:T(8,128)(2,1)} %bitcast.22) | data formatting | bytes 2097152

commit v4 on v3

--- a/solution.py
+++ b/solution.py
@@ -64,23 +64,20 @@
         return pltpu.make_async_copy(srcs[which].at[rows, :], w_buf.at[rows, pl.ds(which * FLAT, FLAT)],
                                      w_sem.at[chunk, which])
 
-    def in_copy(src, buf, sem, head):
-        return pltpu.make_async_copy(src.at[:, head], buf.at[head], sem.at[head])
-
-    def out_copy(buf, dst, sem, head):
-        return pltpu.make_async_copy(buf.at[head], dst.at[:, head], sem.at[head])
-
-    for chunk in range(N_CHUNK):
+    def span(group):
+        return pl.ds(pl.multiple_of(group * 8, 8), 8)
+
+    def in_copy(src, buf, sem, group):
+        return pltpu.make_async_copy(src.at[span(group)], buf.at[span(group)], sem.at[group])
+
+    def out_copy(buf, dst, sem, group):
+        return pltpu.make_async_copy(buf.at[span(group)], dst.at[span(group)], sem.at[group])
+
+    for chunk in range(1):
         for which in range(3):
             w_copy(chunk, which).start()
 
-    def start_in(head, carry):
-        in_copy(sk, k_buf, k_sem, head).start()
-        in_copy(sv, v_buf, v_sem, head).start()
-        return carry
-    lax.fori_loop(0, HEADS, start_in, 0)
     wo_copy = pltpu.make_async_copy(wo, wo_buf, wo_sem)
-    wo_copy.start()
 
     tok_row = tok_ref[...]
     for head, table in enumerate(bias_table(rel_ref[...], tok_row)):
@@ -88,6 +85,9 @@
 
     norm_row[...] = lane_row(norm_ref[...])
     x_copy.wait()
+    for chunk in range(1, N_CHUNK):
+        for which in range(3):
+            w_copy(chunk, which).start()
 
     def norm_rows(step, carry):
         rows = pl.ds(pl.multiple_of(step * 16, 16), 16)
@@ -103,6 +103,13 @@
             rows = pl.ds(pl.multiple_of(chunk * K_CHUNK, K_CHUNK), K_CHUNK)
             cols = slice(which * FLAT, (which + 1) * FLAT)
             acc[:, cols] += jnp.dot(h_buf[:, rows], w_buf[rows, cols], preferred_element_type=F32)
+
+        @pl.when(chunk == 0)
+        def _():
+            for src, buf, sem in ((sk, k_buf, k_sem), (sv, v_buf, v_sem)):
+                for group in range(T_LEN // 8):
+                    in_copy(src, buf, sem, group).start()
+            wo_copy.start()
         return carry
     lax.fori_loop(0, N_CHUNK, qkv_step, 0)
 
@@ -114,48 +121,55 @@
 
     tok_b = jnp.broadcast_to(tok_row.astype(F32), (HEAD_DIM, ROWS)).astype(BF16)
 
-    def start_out(head, carry):
-        out_copy(k_buf, nk, ko_sem, head).start()
-        out_copy(v_buf, nv, vo_sem, head).start()
-        return carry
-
-    def head_step(head, carry):
-        lanes = pl.ds(pl.multiple_of(head * HEAD_DIM, HEAD_DIM), HEAD_DIM)
-        in_copy(sk, k_buf, k_sem, head).wait()
-        query = q_t[lanes, :]
-        fresh_k = kn_t[lanes, :]
-
-        def score_group(group, inner):
-            at_tok = tok_b - (group * 8).astype(F32).astype(BF16)
+    def score_group(group, carry):
+        in_copy(sk, k_buf, k_sem, group).wait()
+        at_tok = tok_b - (group * 8).astype(F32).astype(BF16)
+
+        def per_head(head, inner):
+            lanes = pl.ds(pl.multiple_of(head * HEAD_DIM, HEAD_DIM), HEAD_DIM)
+            query = q_t[lanes, :]
+            fresh_k = kn_t[lanes, :]
             rows = []
             for i in range(8):
                 step = group * 8 + i
-                keys = jnp.where(at_tok == jnp.asarray(i, BF16), fresh_k, k_buf[head, step])
-                k_buf[head, step] = keys
+                keys = jnp.where(at_tok == jnp.asarray(i, BF16), fresh_k, k_buf[step, head])
+                k_buf[step, head] = keys
                 rows.append(jnp.sum(keys.astype(F32) * query, axis=0, keepdims=True))
-            probs[pl.ds(pl.multiple_of(group * 8, 8), 8), :] = jnp.concatenate(rows, axis=0)
+            probs[head, span(group), :] = jnp.concatenate(rows, axis=0)
             return inner
-        lax.fori_loop(0, T_LEN // 8, score_group, 0)
-        scores = probs[...] + bias[head]
+        lax.fori_loop(0, HEADS, per_head, 0)
+        out_copy(k_buf, nk, ko_sem, group).start()
+        return carry
+    lax.fori_loop(0, T_LEN // 8, score_group, 0)
+
+    def soften(head, carry):
+        scores = probs[head] + bias[head]
         weights = jnp.exp(scores - jnp.max(scores, axis=0, keepdims=True))
         weights = weights / jnp.sum(weights, axis=0, keepdims=True)
-        probs[...] = weights.astype(BF16).astype(F32)
-        in_copy(sv, v_buf, v_sem, head).wait()
-        fresh_v = vn_t[lanes, :]
-
-        def mix_group(group, total):
-            at_tok = tok_b - (group * 8).astype(F32).astype(BF16)
+        probs[head] = weights.astype(BF16).astype(F32)
+        return carry
+    lax.fori_loop(0, HEADS, soften, 0)
+    mix[...] = jnp.zeros_like(mix)
+
+    def mix_group(group, carry):
+        in_copy(sv, v_buf, v_sem, group).wait()
+        at_tok = tok_b - (group * 8).astype(F32).astype(BF16)
+
+        def per_head(head, inner):
+            lanes = pl.ds(pl.multiple_of(head * HEAD_DIM, HEAD_DIM), HEAD_DIM)
+            fresh_v = vn_t[lanes, :]
+            total = mix[lanes, :]
             for i in range(8):
                 step = group * 8 + i
-                vals = jnp.where(at_tok == jnp.asarray(i, BF16), fresh_v, v_buf[head, step])
-                v_buf[head, step] = vals
-                total = total + vals.astype(F32) * probs[pl.ds(step, 1), :]
-            return total
-        mix[lanes, :] = lax.fori_loop(0, T_LEN // 8, mix_group, jnp.zeros((HEAD_DIM, ROWS), F32))
-
-        start_out(head, 0)
-        return carry
-    lax.fori_loop(0, HEADS, head_step, 0)
+                vals = jnp.where(at_tok == jnp.asarray(i, BF16), fresh_v, v_buf[step, head])
+                v_buf[step, head] = vals
+                total = total + vals.astype(F32) * probs[head, pl.ds(step, 1), :]
+            mix[lanes, :] = total
+            return inner
+        lax.fori_loop(0, HEADS, per_head, 0)
+        out_copy(v_buf, nv, vo_sem, group).start()
+        return carry
+    lax.fori_loop(0, T_LEN // 8, mix_group, 0)
 
     mixed = jnp.concatenate([jnp.transpose(mix[block * 128:(block + 1) * 128, :]).astype(BF16)
                              for block in range(FLAT // 128)], axis=1)
@@ -185,10 +199,10 @@
         scratch_shapes=[
             pltpu.VMEM((ROWS, D_MODEL), BF16), pltpu.VMEM((ROWS, D_MODEL), BF16),
             pltpu.VMEM((D_MODEL, 3 * FLAT), BF16), pltpu.VMEM((FLAT, D_MODEL), BF16),
-            pltpu.VMEM((HEADS, T_LEN, HEAD_DIM, ROWS), BF16), pltpu.VMEM((HEADS, T_LEN, HEAD_DIM, ROWS), BF16),
+            pltpu.VMEM((T_LEN, HEADS, HEAD_DIM, ROWS), BF16), pltpu.VMEM((T_LEN, HEADS, HEAD_DIM, ROWS), BF16),
             pltpu.VMEM((ROWS, 3 * FLAT), F32), pltpu.VMEM((FLAT, ROWS), F32),
             pltpu.VMEM((FLAT, ROWS), BF16), pltpu.VMEM((FLAT, ROWS), BF16),
-            pltpu.VMEM((HEADS, T_LEN, ROWS), F32), pltpu.VMEM((T_LEN, ROWS), F32), pltpu.VMEM((FLAT, ROWS), F32),
+            pltpu.VMEM((HEADS, T_LEN, ROWS), F32), pltpu.VMEM((HEADS, T_LEN, ROWS), F32), pltpu.VMEM((FLAT, ROWS), F32),
             pltpu.VMEM((1, D_MODEL), F32),
             dma, dma((N_CHUNK, 3)), dma, dma((HEADS,)), dma((HEADS,)), dma((HEADS,)), dma((HEADS,)),
         ],
@@ -203,6 +217,7 @@
 OWN = GROUP_ROWS // 8
 STEP_ROWS = 16
 SPLIT = 2
+BUNDLE = 2
 OUT_COLS = D_MODEL // SPLIT
 STEPS = ROWS // STEP_ROWS
 GROUP_STEPS = STEPS // GROUPS
@@ -211,11 +226,11 @@
 MESH = pl.DeviceIdType.MESH
 
 
-def layer_kernel(part_in, x_hbm, enc_ref, nc_ref, nm_ref, ck, cv, wcq, wco, wg, wu, wd,
-                 out_ref,
+def layer_kernel(part_hbm, x_hbm, enc_ref, nc_ref, nm_ref, ck, cv, wcq, wco, wg, wu, wd,
+                 out_hbm,
                  x_own, g_buf, u_buf, d_buf, co_buf, k_buf, v_buf, part, d2d_buf, chip_sum, rs_buf, h_full,
                  h_rows, resid, q_buf, mixed, hidden, mask_buf, norm_rows,
-                 x_sem, cq_sem, co_sem, g_sem, u_sem, d_sem, k_sem, v_sem,
+                 p_sem, o_sem, x_sem, cq_sem, co_sem, g_sem, u_sem, d_sem, k_sem, v_sem,
                  dd_send, dd_recv, rs_send, rs_recv, ag_send, ag_recv, fw_send, fw_recv):
     me = lax.axis_index('tp')
     core = me % 2
@@ -250,7 +265,9 @@
             copy.start()
         return carry
 
-    for copy in x_copies:
+    part_copies = [pltpu.make_async_copy(part_hbm.at[pl.ds(g * 8, 8)], part.at[pl.ds(g * 8, 8)], p_sem.at[g]) for g in range(GROUPS)]
+    out_copies = [pltpu.make_async_copy(h_full.at[pl.ds(g * 8, 8)], out_hbm.at[pl.ds(g * 8, 8)], o_sem.at[g]) for g in range(GROUPS)]
+    for copy in part_copies + x_copies:
         copy.start()
     cq_copy.start()
     lax.fori_loop(0, SLOTS, kv_start, 0)
@@ -279,18 +296,16 @@
             send_sem=rs_send.at[group, j, part_no], recv_sem=rs_recv.at[group, j, part_no],
             device_id={'tp': peers[j]}, device_id_type=MESH)
 
-    def gather(group, j, rows_ref):
-        own = block(group, core, chip)
+    def gather(group, j, part_no):
+        piece = h_full.at[block(group, core, chip), :, columns(part_no)]
         return pltpu.make_async_remote_copy(
-            src_ref=rows_ref.at[own], dst_ref=rows_ref.at[own],
-            send_sem=ag_send.at[group, j], recv_sem=ag_recv.at[group, j],
+            src_ref=piece, dst_ref=piece, send_sem=ag_send.at[group, j, part_no], recv_sem=ag_recv.at[group, j, part_no],
             device_id={'tp': peers[j]}, device_id_type=MESH)
 
-    def forward(group, j, rows_ref):
-        piece = block(group, core, chip if j == 3 else chips[j])
+    def forward(group, j, part_no):
+        piece = h_full.at[block(group, core, chip if j == 3 else chips[j]), :, columns(part_no)]
         return pltpu.make_async_remote_copy(
-            src_ref=rows_ref.at[piece], dst_ref=rows_ref.at[piece],
-            send_sem=fw_send.at[group, j], recv_sem=fw_recv.at[group, j],
+            src_ref=piece, dst_ref=piece, send_sem=fw_send.at[group, j, part_no], recv_sem=fw_recv.at[group, j, part_no],
             device_id={'tp': partner}, device_id_type=MESH)
 
     def d2d_start(group, src):
@@ -307,29 +322,39 @@
             for j in (2, 0, 1):
                 scatter(group, j, part_no).start()
 
+    def send_rows(group, part_no):
+        for j in (2, 0, 1):
+            gather(group, j, part_no).start()
+        forward(group, 3, part_no).start()
+
     def finish_rows(group, norm, last):
+        own = block(group, core, chip)
         for part_no in range(SPLIT):
             cols = columns(part_no)
             total = resid[group, :, cols] + chip_sum[group, chip, :, cols].astype(F32)
             for j in range(3):
                 scatter(group, j, part_no).wait()
                 total = total + rs_buf[group, j, :, cols].astype(F32)
-            resid[group, :, cols] = total
-        own = block(group, core, chip)
-        rows_ref = out_ref if last else h_full
-        rows_ref[own] = resid[group].astype(BF16) if last else rms_norm(resid[group], norm_rows[norm])
-        for j in (2, 0, 1):
-            gather(group, j, rows_ref).start()
-        forward(group, 3, rows_ref).start()
-
-    def pass_on(group, rows_ref=h_full):
-        for j in (0, 1, 2):
-            gather(group, j, rows_ref).wait()
-            forward(group, j, rows_ref).start()
-
-    def rows_ready(group, rows_ref=h_full):
-        for j in (3, 0, 1, 2):
-            forward(group, j, rows_ref).wait()
+            if last:
+                h_full[own, :, cols] = total.astype(BF16)
+                send_rows(group, part_no)
+            else:
+                resid[group, :, cols] = total
+        if not last:
+            h_full[own] = rms_norm(resid[group], norm_rows[norm])
+            for part_no in range(SPLIT):
+                send_rows(group, part_no)
+
+    def pass_on(group):
+        for part_no in range(SPLIT):
+            for j in (0, 1, 2):
+                gather(group, j, part_no).wait()
+                forward(group, j, part_no).start()
+
+    def rows_ready(group):
+        for part_no in range(SPLIT):
+            for j in (3, 0, 1, 2):
+                forward(group, j, part_no).wait()
 
     def collect(group):
         rows_ready(group)
@@ -358,33 +383,38 @@
 
     def cross_step(step):
         slot = step % SLOTS
-        k_copy, v_copy = kv_copies(step)
-        k_copy.wait()
+        for copy in kv_copies(step):
+            copy.wait()
         base = pl.multiple_of(step * STEP_ROWS, STEP_ROWS)
         q_rows = q_buf[pl.ds(base, STEP_ROWS), :]
         mask_rows = mask_buf[pl.ds(base, STEP_ROWS), :]
-        scores = []
-        for pair in range(STEP_ROWS // 2):
-            left = jnp.concatenate([jnp.where(own_head, q_rows[2 * pair + i:2 * pair + i + 1, :], 0.0) for i in range(2)], axis=0)
-            keys = jnp.concatenate([k_buf[slot, (2 * pair + i) * FLAT:(2 * pair + i + 1) * FLAT, :] for i in range(2)], axis=1)
-            both = jnp.dot(left.astype(BF16), keys, preferred_element_type=F32)
-            scores.append(both[:HEADS, :S_LEN] + mask_rows[2 * pair:2 * pair + 1, :])
-            scores.append(both[HEADS:, S_LEN:] + mask_rows[2 * pair + 1:2 * pair + 2, :])
-        score = jnp.concatenate(scores, axis=0)
-        weight = jnp.exp(score - jnp.max(score, axis=1, keepdims=True))
-        weight = weight / jnp.sum(weight, axis=1, keepdims=True)
-        v_copy.wait()
         zeros = jnp.zeros((HEADS, S_LEN), F32)
+        bundles = [range(first, first + BUNDLE) for first in range(0, STEP_ROWS // 2, BUNDLE)]
+
+        def two(buf, pair):
+            return jnp.concatenate([buf[slot, (2 * pair + i) * FLAT:(2 * pair + i + 1) * FLAT, :] for i in range(2)], axis=1)
+
+        all_scores = []
+        for pairs in bundles:
+            scores = []
+            for pair in pairs:
+                left = jnp.concatenate([jnp.where(own_head, q_rows[2 * pair + i:2 * pair + i + 1, :], 0.0) for i in range(2)], axis=0)
+                both = jnp.dot(left.astype(BF16), two(k_buf, pair), preferred_element_type=F32)
+                scores.append(both[:HEADS, :S_LEN] + mask_rows[2 * pair:2 * pair + 1, :])
+                scores.append(both[HEADS:, S_LEN:] + mask_rows[2 * pair + 1:2 * pair + 2, :])
+            all_scores.append(jnp.concatenate(scores, axis=0))
         rows = []
-        for pair in range(STEP_ROWS // 2):
-            first = weight[2 * pair * HEADS:(2 * pair + 1) * HEADS, :]
-            second = weight[(2 * pair + 1) * HEADS:(2 * pair + 2) * HEADS, :]
-            left = jnp.concatenate([jnp.concatenate([first, zeros], axis=1), jnp.concatenate([zeros, second], axis=1)], axis=0)
-            vals = jnp.concatenate([v_buf[slot, (2 * pair + i) * FLAT:(2 * pair + i + 1) * FLAT, :] for i in range(2)], axis=1)
-            both = lax.dot_general(left.astype(BF16), vals, (((1,), (1,)), ((), ())), preferred_element_type=F32)
-            for i in range(2):
-                mine = jnp.where(own_head, both[i * HEADS:(i + 1) * HEADS, :], 0.0)
-                rows.append(jnp.sum(mine, axis=0, keepdims=True))
+        for pairs, score in zip(bundles, all_scores):
+            weight = jnp.exp(score - jnp.max(score, axis=1, keepdims=True))
+            weight = weight / jnp.sum(weight, axis=1, keepdims=True)
+            for k, pair in enumerate(pairs):
+                first = weight[2 * k * HEADS:(2 * k + 1) * HEADS, :]
+                second = weight[(2 * k + 1) * HEADS:(2 * k + 2) * HEADS, :]
+                left = jnp.concatenate([jnp.concatenate([first, zeros], axis=1), jnp.concatenate([zeros, second], axis=1)], axis=0)
+                both = lax.dot_general(left.astype(BF16), two(v_buf, pair), (((1,), (1,)), ((), ())), preferred_element_type=F32)
+                for i in range(2):
+                    mine = jnp.where(own_head, both[i * HEADS:(i + 1) * HEADS, :], 0.0)
+                    rows.append(jnp.sum(mine, axis=0, keepdims=True))
         mixed[pl.ds(base, STEP_ROWS), :] = jnp.concatenate(rows, axis=0)
 
     def cross_out(group):
@@ -394,22 +424,21 @@
     def mlp_in(group, at_block):
         span = slice(group * GROUP_ROWS, (group + 1) * GROUP_ROWS)
 
-        def unit_step(i, carry):
+        for i in range(UNITS // 256):
             at_block(i)
-            cols = pl.ds(pl.multiple_of(i * 256, 256), 256)
+            cols = slice(i * 256, (i + 1) * 256)
             gate = jnp.dot(h_rows[span, :], g_buf[:, cols], preferred_element_type=F32)
             up = jnp.dot(h_rows[span, :], u_buf[:, cols], preferred_element_type=F32)
             hidden[:, cols] = (jax.nn.gelu(gate, approximate=True) * up).astype(BF16)
-            return carry
-        lax.fori_loop(0, UNITS // 256, unit_step, 0)
 
     def mlp_out(group):
         out_product(group, lambda: hidden[...], d_buf)
 
     for g in range(GROUPS):
-        d2d_start(g, part_in)
+        part_copies[g].wait()
+        d2d_start(g, part)
     for g in range(GROUPS):
-        reduce_chip(g, part_in)
+        reduce_chip(g, part)
     for g in range(GROUPS):
         x_copies[g].wait()
         resid[g] = x_own[g].astype(F32)
@@ -421,24 +450,19 @@
 
     def first_group(i, carry):
         cross_step(i)
-
-        @pl.when(i < STEPS - SLOTS)
-        def _():
-            kv_start(i + SLOTS)
-        return carry
-    lax.fori_loop(0, 3, first_group, 0)
+        kv_start(i + SLOTS)
+        return carry
+    lax.fori_loop(0, GROUP_STEPS - 1, first_group, 0)
     pass_on(1)
-    lax.fori_loop(3, GROUP_STEPS, first_group, 0)
+    first_group(GROUP_STEPS - 1, 0)
     co_copy.wait()
     cross_out(0)
     collect(1)
     queries(1)
     g_copy.start()
+    reduce_chip(0, part)
 
     def second_group(i, carry):
-        @pl.when(i == 1)
-        def _():
-            reduce_chip(0, part)
         cross_step(i + GROUP_STEPS)
         return carry
     lax.fori_loop(0, GROUP_STEPS, second_group, 0)
@@ -446,33 +470,29 @@
     finish_rows(0, 1, False)
     reduce_chip(1, part)
     pass_on(0)
+    finish_rows(1, 1, False)
     collect(0)
     g_copy.wait()
     u_copy.wait()
     d_copy.wait()
 
-    def mid_first(i):
-        @pl.when(i == 0)
-        def _():
-            finish_rows(1, 1, False)
-    mlp_in(0, mid_first)
+    mlp_in(0, lambda i: None)
     pass_on(1)
     mlp_out(0)
     collect(1)
-
-    def mid_second(i):
-        @pl.when(i == 1)
-        def _():
-            reduce_chip(0, part)
-    mlp_in(1, mid_second)
+    mlp_in(1, lambda i: reduce_chip(0, part) if i == 1 else None)
     finish_rows(0, 1, True)
     mlp_out(1)
     reduce_chip(1, part)
-    pass_on(0, out_ref)
+    pass_on(0)
     finish_rows(1, 1, True)
-    rows_ready(0, out_ref)
-    pass_on(1, out_ref)
-    rows_ready(1, out_ref)
+    rows_ready(0)
+    out_copies[0].start()
+    pass_on(1)
+    rows_ready(1)
+    out_copies[1].start()
+    for copy in out_copies:
+        copy.wait()
 
 
 def layer_stage(part, x_blocks, enc_mask, norm_cross, norm_mlp, ck, cv, cross_q, cross_o, w_gate, w_up, w_down):
@@ -483,8 +503,8 @@
     return pl.pallas_call(
         layer_kernel,
         out_shape=jax.ShapeDtypeStruct(blocks, BF16),
-        in_specs=[vmem, hbm, vmem, vmem, vmem] + [hbm] * 7,
-        out_specs=vmem,
+        in_specs=[hbm, hbm, vmem, vmem, vmem] + [hbm] * 7,
+        out_specs=hbm,
         scratch_shapes=[
             pltpu.VMEM((GROUPS, OWN, D_MODEL), BF16),
             pltpu.VMEM((D_MODEL, UNITS), BF16), pltpu.VMEM((D_MODEL, UNITS), BF16), pltpu.VMEM((UNITS, D_MODEL), BF16),
@@ -496,10 +516,10 @@
             pltpu.VMEM((ROWS, D_MODEL), BF16), pltpu.VMEM((GROUPS, OWN, D_MODEL), F32),
             pltpu.VMEM((ROWS, FLAT), F32), pltpu.VMEM((ROWS, FLAT), F32), pltpu.VMEM((GROUP_ROWS, UNITS), BF16),
             pltpu.VMEM((ROWS, S_LEN), F32), pltpu.VMEM((2, 1, D_MODEL), F32),
-            dma((GROUPS,)), dma, dma, dma, dma, dma, dma((SLOTS,)), dma((SLOTS,)),
+            dma((GROUPS,)), dma((GROUPS,)), dma((GROUPS,)), dma, dma, dma, dma, dma, dma((SLOTS,)), dma((SLOTS,)),
             dma((GROUPS, SPLIT)), dma((GROUPS, SPLIT)), dma((GROUPS, 3, SPLIT)), dma((GROUPS, 3, SPLIT)),
-            dma((GROUPS, 3)), dma((GROUPS, 3)),
-            dma((GROUPS, 4)), dma((GROUPS, 4)),
+            dma((GROUPS, 3, SPLIT)), dma((GROUPS, 3, SPLIT)),
+            dma((GROUPS, 4, SPLIT)), dma((GROUPS, 4, SPLIT)),
         ],
         compiler_params=pltpu.CompilerParams(collective_id=0, has_side_effects=True, vmem_limit_bytes=59 * 1024 * 1024),
         cost_estimate=pl.CostEstimate(flops=10 ** 10, bytes_accessed=70 * 2 ** 20, transcendentals=0),

time: 90.9 us -> 86.7 us (0.954)
  Pallas kernels: 87.8 us -> 83.5 us
    pallas_call x1, Pallas kernels: 67.2 us -> 64 us  [layer_stage(): pl.pallas_call(layer_kernel, out_shape=jax.ShapeDtypeStruct(blocks, BF16)...]
    pallas_call x1, Pallas kernels: 20.6 us -> 19.5 us  [self_stage(): pl.pallas_call(self_kernel, out_shape=(jax.ShapeDtypeStruct((16, 8, D_MOD...]
where the time goes in v4:
time: 86.7 us; the launch traced here: 86.4 us
  Pallas kernels  83.5 us (96%)
  local copies, waits for them, and re-layouts  2.29 us (3%)
    pallas_call x1, Pallas kernels, layer_stage(): pl.pallas_call(layer_kernel, out_shape=jax.ShapeDtypeStruct(blocks, BF16)...  64 us
    pallas_call x1, Pallas kernels, self_stage(): pl.pallas_call(self_kernel, out_shape=(jax.ShapeDtypeStruct((16, 8, D_MOD...  19.5 us
    unnamed x1, local copies, waits for them, and re-layouts  2.29 us

profile of v4, /device:TPU:0, one launch (start us, length us, event | category | flops | bytes accessed | tf_op | source)
XLA Modules:
  0.0 86.4 jit_solution(10239013540251430658)
XLA Ops:
  0.6 19.5 %self_stage.1 = (bf16[16,8,4096]{2,1,0:T(8,128)(2,1)}, bf16[64,8,64,128]{3,2,1,0:T(8,128)(2,1)}, bf16[64,8,64,128]{3,2,1,0:T(8,128)(2,1)}) custom-call(bf16[128,4096]{1,0:T(8,128)(2,1)} %x_hbm.1, s32[1,128]{1,0:T(1,128)} %bitcast.27, f32[8,32]{1,0:T(8,128)} %bitcast.26, bf16[32,128]{1,0:T(8,128)(2,1)} %bitcast.25, bf16[4096,512]{1,0:T(8,128)(2,1)} %wq.1, ...), custom_call_target="tpu_custom_call" | custom-call | flops 1000000000 | bytes 52428800 | tf_op jit(solution)/shard_map/self_stage/pallas_call | solution.py:194
  20.2 64.0 %layer_stage.1 = bf16[16,8,4096]{2,1,0:T(8,128)(2,1)} custom-call(bf16[16,8,4096]{2,1,0:T(8,128)(2,1)} %get-tuple-element.6.part_hbm, bf16[16,8,4096]{2,1,0:T(8,128)(2,1)} %bitcast.21, s32[128,128]{1,0:T(8,128)} %enc_ref.1, bf16[32,128]{1,0:T(8,128)(2,1)} %bitcast.23, bf16[32,128]{1,0:T(8,128)(2,1)} %bitcast.24, bf16[65536,128]{1,0:T(8,128)(2,1)} %bitcast.17, ...), custom_call_target="tpu_custom_call" | custom-call | flops 10000000000 | bytes 73400320 | tf_op jit(solution)/shard_map/layer_stage/pallas_call | solution.py:503
  84.2 2.3 %copy.24 = bf16[128,4096]{1,0:T(8,128)(2,1)} copy(bf16[128,4096]{1,0:T(8,128)(2,1)} %bitcast.22) | data formatting | bytes 2097152

commit v5 on v4

--- a/solution.py
+++ b/solution.py
@@ -51,12 +51,16 @@
     return tables
 
 
-def self_kernel(x_hbm, tok_ref, rel_ref, norm_ref, wq, wk, wv, wo, sk, sv,
-                part_ref, nk, nv,
-                x_buf, h_buf, w_buf, wo_buf, k_buf, v_buf, acc, q_t, kn_t, vn_t, bias, probs, mix, norm_row,
-                x_sem, w_sem, wo_sem, k_sem, v_sem, ko_sem, vo_sem):
+def self_kernel(x_hbm, tok_hbm, rel_hbm, norm_hbm, wq, wk, wv, wo, sk, sv,
+                part_hbm, nk, nv,
+                x_buf, h_buf, w_buf, wo_buf, k_buf, v_buf, acc, q_t, kn_t, vn_t, bias, probs, mix, norm_row, part_ref,
+                tok_ref, rel_ref, norm_ref, small_sem, part_sem, x_sem, w_sem, wo_sem, k_sem, v_sem, ko_sem, vo_sem):
     x_copy = pltpu.make_async_copy(x_hbm, x_buf, x_sem)
     x_copy.start()
+    small_copies = [pltpu.make_async_copy(src, dst, small_sem.at[i]) for i, (src, dst) in enumerate(
+        ((tok_hbm, tok_ref), (rel_hbm, rel_ref), (norm_hbm, norm_ref)))]
+    for copy in small_copies:
+        copy.start()
     srcs = (wq, wk, wv)
 
     def w_copy(chunk, which):
@@ -79,6 +83,8 @@
 
     wo_copy = pltpu.make_async_copy(wo, wo_buf, wo_sem)
 
+    for copy in small_copies:
+        copy.wait()
     tok_row = tok_ref[...]
     for head, table in enumerate(bias_table(rel_ref[...], tok_row)):
         bias[head] = table
@@ -137,7 +143,7 @@
                 rows.append(jnp.sum(keys.astype(F32) * query, axis=0, keepdims=True))
             probs[head, span(group), :] = jnp.concatenate(rows, axis=0)
             return inner
-        lax.fori_loop(0, HEADS, per_head, 0)
+        lax.fori_loop(0, HEADS, per_head, 0, unroll=4)
         out_copy(k_buf, nk, ko_sem, group).start()
         return carry
     lax.fori_loop(0, T_LEN // 8, score_group, 0)
@@ -166,7 +172,7 @@
                 total = total + vals.astype(F32) * probs[head, pl.ds(step, 1), :]
             mix[lanes, :] = total
             return inner
-        lax.fori_loop(0, HEADS, per_head, 0)
+        lax.fori_loop(0, HEADS, per_head, 0, unroll=4)
         out_copy(v_buf, nv, vo_sem, group).start()
         return carry
     lax.fori_loop(0, T_LEN // 8, mix_group, 0)
@@ -175,9 +181,17 @@
                              for block in range(FLAT // 128)], axis=1)
     wo_copy.wait()
 
+    def part_copy(part_no):
+        cols = pl.ds(part_no * 1024, 1024)
+        return pltpu.make_async_copy(part_ref.at[:, :, cols], part_hbm.at[:, :, cols], part_sem.at[part_no])
+
     for start in range(0, D_MODEL, 1024):
         value = jnp.dot(mixed, wo_buf[:, start:start + 1024], preferred_element_type=F32)
         part_ref[:, :, start:start + 1024] = value.reshape(16, 8, 1024).astype(BF16)
+        part_copy(start // 1024).start()
+
+    for part_no in range(4):
+        part_copy(part_no).wait()
 
     def end_out(head, carry):
         out_copy(k_buf, nk, ko_sem, head).wait()
@@ -188,14 +202,13 @@
 
 def self_stage(x_in, tok_row, rel_t, norm_row, w_q, w_k, w_v, w_o, sk_t, sv_t):
     hbm = pl.BlockSpec(memory_space=pltpu.HBM)
-    vmem = pl.BlockSpec(memory_space=pltpu.VMEM)
     cache = jax.ShapeDtypeStruct((T_LEN, HEADS, HEAD_DIM, ROWS), BF16)
     dma = pltpu.SemaphoreType.DMA
     return pl.pallas_call(
         self_kernel,
         out_shape=(jax.ShapeDtypeStruct((16, 8, D_MODEL), BF16), cache, cache),
-        in_specs=[hbm, vmem, vmem, vmem] + [hbm] * 6,
-        out_specs=(vmem, hbm, hbm),
+        in_specs=[hbm] * 10,
+        out_specs=(hbm, hbm, hbm),
         scratch_shapes=[
             pltpu.VMEM((ROWS, D_MODEL), BF16), pltpu.VMEM((ROWS, D_MODEL), BF16),
             pltpu.VMEM((D_MODEL, 3 * FLAT), BF16), pltpu.VMEM((FLAT, D_MODEL), BF16),
@@ -203,8 +216,9 @@
             pltpu.VMEM((ROWS, 3 * FLAT), F32), pltpu.VMEM((FLAT, ROWS), F32),
             pltpu.VMEM((FLAT, ROWS), BF16), pltpu.VMEM((FLAT, ROWS), BF16),
             pltpu.VMEM((HEADS, T_LEN, ROWS), F32), pltpu.VMEM((HEADS, T_LEN, ROWS), F32), pltpu.VMEM((FLAT, ROWS), F32),
-            pltpu.VMEM((1, D_MODEL), F32),
-            dma, dma((N_CHUNK, 3)), dma, dma((HEADS,)), dma((HEADS,)), dma((HEADS,)), dma((HEADS,)),
+            pltpu.VMEM((1, D_MODEL), F32), pltpu.VMEM((16, 8, D_MODEL), BF16),
+            pltpu.VMEM((1, ROWS), jnp.int32), pltpu.VMEM((HEADS, 32), F32), pltpu.VMEM((32, 128), BF16), dma((3,)),
+            dma((4,)), dma, dma((N_CHUNK, 3)), dma, dma((HEADS,)), dma((HEADS,)), dma((HEADS,)), dma((HEADS,)),
         ],
         compiler_params=pltpu.CompilerParams(vmem_limit_bytes=60 * 1024 * 1024),
         cost_estimate=pl.CostEstimate(flops=10 ** 9, bytes_accessed=50 * 2 ** 20, transcendentals=0),
@@ -226,11 +240,11 @@
 MESH = pl.DeviceIdType.MESH
 
 
-def layer_kernel(part_hbm, x_hbm, enc_ref, nc_ref, nm_ref, ck, cv, wcq, wco, wg, wu, wd,
+def layer_kernel(part_hbm, x_hbm, enc_hbm, nc_hbm, nm_hbm, ck, cv, wcq, wco, wg, wu, wd,
                  out_hbm,
                  x_own, g_buf, u_buf, d_buf, co_buf, k_buf, v_buf, part, d2d_buf, chip_sum, rs_buf, h_full,
                  h_rows, resid, q_buf, mixed, hidden, mask_buf, norm_rows,
-                 p_sem, o_sem, x_sem, cq_sem, co_sem, g_sem, u_sem, d_sem, k_sem, v_sem,
+                 enc_ref, nc_ref, nm_ref, small_sem, p_sem, o_sem, x_sem, cq_sem, co_sem, g_sem, u_sem, d_sem, k_sem, v_sem,
                  dd_send, dd_recv, rs_send, rs_recv, ag_send, ag_recv, fw_send, fw_recv):
     me = lax.axis_index('tp')
     core = me % 2
@@ -267,7 +281,9 @@
 
     part_copies = [pltpu.make_async_copy(part_hbm.at[pl.ds(g * 8, 8)], part.at[pl.ds(g * 8, 8)], p_sem.at[g]) for g in range(GROUPS)]
     out_copies = [pltpu.make_async_copy(h_full.at[pl.ds(g * 8, 8)], out_hbm.at[pl.ds(g * 8, 8)], o_sem.at[g]) for g in range(GROUPS)]
-    for copy in part_copies + x_copies:
+    small_copies = [pltpu.make_async_copy(src, dst, small_sem.at[i]) for i, (src, dst) in enumerate(
+        ((enc_hbm, enc_ref), (nc_hbm, nc_ref), (nm_hbm, nm_ref)))]
+    for copy in part_copies + x_copies + small_copies:
         copy.start()
     cq_copy.start()
     lax.fori_loop(0, SLOTS, kv_start, 0)
@@ -275,9 +291,6 @@
     u_copy.start()
     d_copy.start()
 
-    norm_rows[0] = lane_row(nc_ref[...])
-    norm_rows[1] = lane_row(nm_ref[...])
-    mask_buf[...] = jnp.where(enc_ref[...] != 0, 0.0, NEG_FILL)
     pl.semaphore_wait(barrier, 4)
 
     def columns(part_no):
@@ -437,6 +450,11 @@
     for g in range(GROUPS):
         part_copies[g].wait()
         d2d_start(g, part)
+    for copy in small_copies:
+        copy.wait()
+    norm_rows[0] = lane_row(nc_ref[...])
+    norm_rows[1] = lane_row(nm_ref[...])
+    mask_buf[...] = jnp.where(enc_ref[...] != 0, 0.0, NEG_FILL)
     for g in range(GROUPS):
         reduce_chip(g, part)
     for g in range(GROUPS):
@@ -497,13 +515,12 @@
 
 def layer_stage(part, x_blocks, enc_mask, norm_cross, norm_mlp, ck, cv, cross_q, cross_o, w_gate, w_up, w_down):
     hbm = pl.BlockSpec(memory_space=pltpu.HBM)
-    vmem = pl.BlockSpec(memory_space=pltpu.VMEM)
     dma = pltpu.SemaphoreType.DMA
     blocks = (2 * 8, OWN, D_MODEL)
     return pl.pallas_call(
         layer_kernel,
         out_shape=jax.ShapeDtypeStruct(blocks, BF16),
-        in_specs=[hbm, hbm, vmem, vmem, vmem] + [hbm] * 7,
+        in_specs=[hbm] * 12,
         out_specs=hbm,
         scratch_shapes=[
             pltpu.VMEM((GROUPS, OWN, D_MODEL), BF16),
@@ -516,6 +533,7 @@
             pltpu.VMEM((ROWS, D_MODEL), BF16), pltpu.VMEM((GROUPS, OWN, D_MODEL), F32),
             pltpu.VMEM((ROWS, FLAT), F32), pltpu.VMEM((ROWS, FLAT), F32), pltpu.VMEM((GROUP_ROWS, UNITS), BF16),
             pltpu.VMEM((ROWS, S_LEN), F32), pltpu.VMEM((2, 1, D_MODEL), F32),
+            pltpu.VMEM((ROWS, S_LEN), jnp.int32), pltpu.VMEM((32, 128), BF16), pltpu.VMEM((32, 128), BF16), dma((3,)),
             dma((GROUPS,)), dma((GROUPS,)), dma((GROUPS,)), dma, dma, dma, dma, dma, dma((SLOTS,)), dma((SLOTS,)),
             dma((GROUPS, SPLIT)), dma((GROUPS, SPLIT)), dma((GROUPS, 3, SPLIT)), dma((GROUPS, 3, SPLIT)),
             dma((GROUPS, 3, SPLIT)), dma((GROUPS, 3, SPLIT)),

time: 86.7 us -> 84.5 us (0.975)
  Pallas kernels: 83.5 us -> 81.4 us
    pallas_call x1, Pallas kernels: 19.5 us -> 18.2 us  [self_stage(): pl.pallas_call(self_kernel, out_shape=(jax.ShapeDtypeStruct((16, 8, D_MOD...]
where the time goes in v5:
time: 84.5 us; the launch traced here: 84.4 us
  Pallas kernels  81.4 us (96%)
  local copies, waits for them, and re-layouts  2.29 us (3%)
    pallas_call x1, Pallas kernels, layer_stage(): pl.pallas_call(layer_kernel, out_shape=jax.ShapeDtypeStruct(blocks, BF16)...  63.2 us
    pallas_call x1, Pallas kernels, self_stage(): pl.pallas_call(self_kernel, out_shape=(jax.ShapeDtypeStruct((16, 8, D_MOD...  18.2 us
    unnamed x1, local copies, waits for them, and re-layouts  2.29 us

profile of v5, /device:TPU:0, one launch (start us, length us, event | category | flops | bytes accessed | tf_op | source)
XLA Modules:
  0.0 84.4 jit_solution(13842791857163981845)
XLA Ops:
  0.6 18.2 %self_stage.1 = (bf16[16,8,4096]{2,1,0:T(8,128)(2,1)}, bf16[64,8,64,128]{3,2,1,0:T(8,128)(2,1)}, bf16[64,8,64,128]{3,2,1,0:T(8,128)(2,1)}) custom-call(bf16[128,4096]{1,0:T(8,128)(2,1)} %x_hbm.1, s32[1,128]{1,0:T(1,128)} %bitcast.27, f32[8,32]{1,0:T(8,128)} %bitcast.26, bf16[32,128]{1,0:T(8,128)(2,1)} %bitcast.25, bf16[4096,512]{1,0:T(8,128)(2,1)} %wq.1, ...), custom_call_target="tpu_custom_call" | custom-call | flops 1000000000 | bytes 52428800 | tf_op jit(solution)/shard_map/self_stage/pallas_call | solution.py:207
  18.9 63.2 %layer_stage.1 = bf16[16,8,4096]{2,1,0:T(8,128)(2,1)} custom-call(bf16[16,8,4096]{2,1,0:T(8,128)(2,1)} %get-tuple-element.6.part_hbm, bf16[16,8,4096]{2,1,0:T(8,128)(2,1)} %bitcast.21, s32[128,128]{1,0:T(8,128)} %enc_hbm.1, bf16[32,128]{1,0:T(8,128)(2,1)} %bitcast.23, bf16[32,128]{1,0:T(8,128)(2,1)} %bitcast.24, bf16[65536,128]{1,0:T(8,128)(2,1)} %bitcast.17, ...), custom_call_target="tpu_custom_call" | custom-call | flops 10000000000 | bytes 73400320 | tf_op jit(solution)/shard_map/layer_stage/pallas_call | solution.py:520
  82.1 2.3 %copy.24 = bf16[128,4096]{1,0:T(8,128)(2,1)} copy(bf16[128,4096]{1,0:T(8,128)(2,1)} %bitcast.22) | data formatting | bytes 2097152

commit v6 on v5

--- a/solution.py
+++ b/solution.py
@@ -77,7 +77,7 @@
     def out_copy(buf, dst, sem, group):
         return pltpu.make_async_copy(buf.at[span(group)], dst.at[span(group)], sem.at[group])
 
-    for chunk in range(1):
+    for chunk in range(2):
         for which in range(3):
             w_copy(chunk, which).start()
 
@@ -91,7 +91,7 @@
 
     norm_row[...] = lane_row(norm_ref[...])
     x_copy.wait()
-    for chunk in range(1, N_CHUNK):
+    for chunk in range(2, N_CHUNK):
         for which in range(3):
             w_copy(chunk, which).start()
 
@@ -154,7 +154,7 @@
         weights = weights / jnp.sum(weights, axis=0, keepdims=True)
         probs[head] = weights.astype(BF16).astype(F32)
         return carry
-    lax.fori_loop(0, HEADS, soften, 0)
+    lax.fori_loop(0, HEADS, soften, 0, unroll=8)
     mix[...] = jnp.zeros_like(mix)
 
     def mix_group(group, carry):
@@ -285,11 +285,6 @@
         ((enc_hbm, enc_ref), (nc_hbm, nc_ref), (nm_hbm, nm_ref)))]
     for copy in part_copies + x_copies + small_copies:
         copy.start()
-    cq_copy.start()
-    lax.fori_loop(0, SLOTS, kv_start, 0)
-    co_copy.start()
-    u_copy.start()
-    d_copy.start()
 
     pl.semaphore_wait(barrier, 4)
 
@@ -450,6 +445,11 @@
     for g in range(GROUPS):
         part_copies[g].wait()
         d2d_start(g, part)
+    cq_copy.start()
+    lax.fori_loop(0, SLOTS, kv_start, 0)
+    co_copy.start()
+    u_copy.start()
+    d_copy.start()
     for copy in small_copies:
         copy.wait()
     norm_rows[0] = lane_row(nc_ref[...])
@@ -471,8 +471,8 @@
         kv_start(i + SLOTS)
         return carry
     lax.fori_loop(0, GROUP_STEPS - 1, first_group, 0)
+    first_group(GROUP_STEPS - 1, 0)
     pass_on(1)
-    first_group(GROUP_STEPS - 1, 0)
     co_copy.wait()
     cross_out(0)
     collect(1)

time: 84.5 us -> 84.4 us (level)
  no operation moved by 1% of the time
where the time goes in v6:
time: 84.4 us; the launch traced here: 84.3 us
  Pallas kernels  81.4 us (96%)
  local copies, waits for them, and re-layouts  2.29 us (3%)
    pallas_call x1, Pallas kernels, layer_stage(): pl.pallas_call(layer_kernel, out_shape=jax.ShapeDtypeStruct(blocks, BF16)...  63.3 us
    pallas_call x1, Pallas kernels, self_stage(): pl.pallas_call(self_kernel, out_shape=(jax.ShapeDtypeStruct((16, 8, D_MOD...  18.1 us
    unnamed x1, local copies, waits for them, and re-layouts  2.29 us

profile of v6, /device:TPU:0, one launch (start us, length us, event | category | flops | bytes accessed | tf_op | source)
XLA Modules:
  0.0 84.3 jit_solution(13231962222574084367)
XLA Ops:
  0.6 18.1 %self_stage.1 = (bf16[16,8,4096]{2,1,0:T(8,128)(2,1)}, bf16[64,8,64,128]{3,2,1,0:T(8,128)(2,1)}, bf16[64,8,64,128]{3,2,1,0:T(8,128)(2,1)}) custom-call(bf16[128,4096]{1,0:T(8,128)(2,1)} %x_hbm.1, s32[1,128]{1,0:T(1,128)} %bitcast.27, f32[8,32]{1,0:T(8,128)} %bitcast.26, bf16[32,128]{1,0:T(8,128)(2,1)} %bitcast.25, bf16[4096,512]{1,0:T(8,128)(2,1)} %wq.1, ...), custom_call_target="tpu_custom_call" | custom-call | flops 1000000000 | bytes 52428800 | tf_op jit(solution)/shard_map/self_stage/pallas_call | solution.py:207
  18.7 63.3 %layer_stage.1 = bf16[16,8,4096]{2,1,0:T(8,128)(2,1)} custom-call(bf16[16,8,4096]{2,1,0:T(8,128)(2,1)} %get-tuple-element.6.part_hbm, bf16[16,8,4096]{2,1,0:T(8,128)(2,1)} %bitcast.21, s32[128,128]{1,0:T(8,128)} %enc_hbm.1, bf16[32,128]{1,0:T(8,128)(2,1)} %bitcast.23, bf16[32,128]{1,0:T(8,128)(2,1)} %bitcast.24, bf16[65536,128]{1,0:T(8,128)(2,1)} %bitcast.17, ...), custom_call_target="tpu_custom_call" | custom-call | flops 10000000000 | bytes 73400320 | tf_op jit(solution)/shard_map/layer_stage/pallas_call | solution.py:520
  82.0 2.3 %copy.24 = bf16[128,4096]{1,0:T(8,128)(2,1)} copy(bf16[128,4096]{1,0:T(8,128)(2,1)} %bitcast.22) | data formatting | bytes 2097152
